TPU v7x, 16 devices: a whole 2x2x2 slice. The times are simulated.
16 devices in a mesh: dp: 2 (over z), ep: 8 (over y, x, core).
Axes of the slice: x: 2, y: 2, z: 2, core: 2. Of those that a mesh axis runs over, the one named last changes fastest.
Arguments:
- x: bfloat16 [32768, 2048], P(('dp', 'ep')), parts along dimension 0
- route_idx: int32 [32768, 8], P(('dp', 'ep')), parts along dimension 0
- gates: bfloat16 [32768, 8], P(('dp', 'ep')), parts along dimension 0
- w1: bfloat16 [72, 2048, 1024], P('ep')
- w3: bfloat16 [72, 2048, 1024], P('ep')
- w2: bfloat16 [72, 1024, 2048], P('ep')
Outputs:
- output: bfloat16 [32768, 2048], P(('dp', 'ep')), parts along dimension 0
There are 2 independent parts. A program takes and returns all parts, laid end to end along the dimension named above; an argument that names none is the same for every part.
All inputs are finite; a program needn't handle non-finite values.
Results may differ from a plain program's by a relative error of at most 0.0014.
Values are sent between devices in bfloat16 or wider.
A program may use at most 1 GiB of HBM per device.

v0:
```python
import jax
import jax.numpy as jnp
from jax import lax
from jax.sharding import PartitionSpec as P

BLK = 128


def holder_list(p):
    return [0, (p // 2 + 1) % p, (p // 4 + 2) % p, (3 * p // 4 + 3) % p]


def counting(ids, ng):
    n = ids.shape[0]
    nb = -(-n // BLK)
    idp = jnp.pad(ids, (0, nb * BLK - n), constant_values=ng).reshape(nb, BLK, 1)
    oh = (idp == jnp.arange(ng, dtype=ids.dtype)).astype(jnp.bfloat16)
    tri = (jnp.arange(BLK)[:, None] > jnp.arange(BLK)[None, :]).astype(jnp.bfloat16)
    inb = jnp.einsum("ij,bjg->big", tri, oh, preferred_element_type=jnp.float32)
    ohf = oh.astype(jnp.float32)
    tot = jnp.sum(ohf, axis=1)
    cnt = jnp.sum(tot, axis=0)
    r = inb + (jnp.cumsum(tot, axis=0) - tot)[:, None, :]
    rank = jnp.sum(r * ohf, axis=2).reshape(-1)[:n]
    pos = jnp.sum((r + (jnp.cumsum(cnt) - cnt)) * ohf, axis=2).reshape(-1)[:n]
    return rank.astype(jnp.int32), pos.astype(jnp.int32), cnt.astype(jnp.int32)


def grouped_ffn(rows, gid, w1, w3, w2):
    n, d = rows.shape
    g = w1.shape[0]
    _, pos, cnt = counting(gid, g + 1)
    q = jnp.arange(n, dtype=jnp.int32)
    perm = jnp.sum(jnp.where(pos[:, None] == q[None, :], q[:, None], 0), axis=0)
    xs = rows[perm]
    gs = cnt[:g]
    u = lax.ragged_dot(xs, w1, gs, preferred_element_type=jnp.float32)
    v = lax.ragged_dot(xs, w3, gs, preferred_element_type=jnp.float32)
    a = (jax.nn.silu(u) * v).astype(jnp.bfloat16)
    o = lax.ragged_dot(a, w2, gs, preferred_element_type=jnp.float32).astype(jnp.bfloat16)
    return jnp.where((gid < g)[:, None], o[pos], jnp.zeros((), jnp.bfloat16))


def plan_source(ridx, p, loc, nh):
    td, k = ridx.shape
    e = ridx.reshape(-1)
    hot = e == 0
    dest = e // loc
    capc = td * k // p
    caph = -(-td // nh)
    rank, _, _ = counting(jnp.where(hot, p, dest), p + 1)
    cpos = jnp.where(hot, p * capc, dest * capc + rank)
    hpos = jnp.where(hot, (rank % nh) * caph + rank // nh, nh * caph)
    return hot, cpos, hpos, e % loc, jnp.sum(hot.astype(jnp.int32))


def pack(x, cpos, hpos, lslot, p, capc, nh, caph, value_a5):
    td, d = x.shape
    k = cpos.shape[0] // td
    cm = cpos.reshape(td, k).T[:, None, :] == jnp.arange(p * capc, dtype=jnp.int32)[None, :, None]
    hm = hpos.reshape(td, k).T[:, None, :] == jnp.arange(nh * caph, dtype=jnp.int32)[None, :, None]
    cgid = value_a5 - jnp.sum(jnp.where(cm, value_a5 - lslot.reshape(td, k).T[:, None, :], 0), axis=(0, 2))
    cbuf = jnp.dot(jnp.sum(cm, axis=0).astype(jnp.bfloat16), x, preferred_element_type=jnp.float32).astype(jnp.bfloat16)
    hbuf = jnp.dot(jnp.sum(hm, axis=0).astype(jnp.bfloat16), x, preferred_element_type=jnp.float32).astype(jnp.bfloat16)
    return cbuf, cgid, hbuf.reshape(nh, caph, d)


def combine(gates, hot, cpos, hpos, cret, hres):
    td, k = gates.shape
    d = cret.shape[1]
    hr = hres.reshape(-1, d)
    gt = gates.T[:, :, None]
    zero = jnp.zeros((), gates.dtype)
    gc = jnp.sum(jnp.where(cpos.reshape(td, k).T[:, :, None] == jnp.arange(cret.shape[0], dtype=jnp.int32), gt, zero), axis=0)
    gh = jnp.sum(jnp.where(hpos.reshape(td, k).T[:, :, None] == jnp.arange(hr.shape[0], dtype=jnp.int32), gt, zero), axis=0)
    y = jnp.dot(gc, cret, preferred_element_type=jnp.float32) + jnp.dot(gh, hr, preferred_element_type=jnp.float32)
    return y.astype(jnp.bfloat16)


def solution(mesh):
    p = mesh.shape["ep"]
    hold = holder_list(p)
    nh = len(hold)
    table = [hold.index(q) if q in hold else nh for q in range(p)]

    def local(x, ridx, gates, w1, w3, w2):
        td, d = x.shape
        k = ridx.shape[1]
        value_a5 = w1.shape[0]
        loc = value_a5 - 1
        capc = td * k // p
        caph = -(-td // nh)
        me = lax.axis_index("ep")
        tab = jnp.array(table, jnp.int32)
        gme = tab[me]
        is_h = gme < nh
        slot_h = jnp.where(me == 0, 0, loc)
        hot, cpos, hpos, lslot, nhot = plan_source(ridx, p, loc, nh)
        cbuf, cgid, hbuf = pack(x, cpos, hpos, lslot, p, capc, nh, caph, value_a5)
        counts = lax.all_gather(nhot, "ep")
        crecv = lax.all_to_all(cbuf, "ep", 0, 0, tiled=True)
        crgid = lax.all_to_all(cgid, "ep", 0, 0, tiled=True)
        hblocks = [hbuf[jnp.minimum(gme, nh - 1)]]
        for dl in range(1, p):
            pairs = [(j, (j + dl) % p) for j in range(p) if (j + dl) % p in hold]
            blk = hbuf[jnp.minimum(tab[(me + dl) % p], nh - 1)]
            hblocks.append(lax.ppermute(blk, "ep", pairs))
        hrecv = jnp.stack(hblocks).reshape(p * caph, d)
        srcs = (me - jnp.arange(p)) % p
        cnt = (counts[srcs] - gme + nh - 1) // nh
        valid = jnp.logical_and(jnp.arange(caph)[None, :] < cnt[:, None], is_h)
        hgid = jnp.where(valid, slot_h, value_a5).reshape(-1)
        out = grouped_ffn(jnp.concatenate([crecv, hrecv], axis=0), jnp.concatenate([crgid, hgid], axis=0), w1, w3, w2)
        cret = lax.all_to_all(out[:p * capc], "ep", 0, 0, tiled=True)
        hout = out[p * capc:].reshape(p, caph, d)
        back = [hout[0]]
        for dl in range(1, p):
            pairs = [((j + dl) % p, j) for j in range(p) if (j + dl) % p in hold]
            back.append(lax.ppermute(hout[dl], "ep", pairs))
        hres = jnp.stack(back)[(jnp.array(hold, jnp.int32) - me) % p]
        return combine(gates, hot, cpos, hpos, cret, hres)

    spec_t = P(("dp", "ep"), None)
    spec_w = P("ep", None, None)
    return jax.shard_map(local, mesh=mesh, in_specs=(spec_t, spec_t, spec_t, spec_w, spec_w, spec_w), out_specs=spec_t, check_vma=False)
```

profile of v0, /device:TPU:0, one launch (start us, length us, event | category | flops | bytes accessed | tf_op | source)
XLA Modules:
  0.0 4710.5 jit_solution(9679605888323194104)
XLA Ops:
  11.0 297.7 %select_reduce_fusion.1 = s32[16384]{0:T(1024)S(1)} fusion(s32[8,2048]{1,0:T(8,128)S(1)} %copy.52, s32[8,2048]{1,0:T(8,128)S(1)} %copy.50), kind=kLoop, calls=%fused_computation.8 | loop fusion | flops 805289984 | bytes 196608 | tf_op jit(solution)/shard_map/reduce_sum | solution.py:62
  315.0 167.8 %convert_reduce_fusion = s32[16384,2048]{1,0:T(8,128)} fusion(s32[8,2048]{1,0:T(8,128)S(1)} %copy.50), kind=kLoop, calls=%fused_computation.7 | loop fusion | flops 771751936 | bytes 134283264 | tf_op jit(solution)/shard_map/reduce_sum | solution.py:63
  483.7 148.9 %fusion.6 = bf16[16384,2048]{1,0:T(8,128)(2,1)} fusion(bf16[2048,2048]{1,0:T(8,128)(2,1)} %param.8, s32[16384,2048]{1,0:T(8,128)} %convert_reduce_fusion), kind=kOutput, calls=%fused_computation.23 | convolution fusion | flops 137506062336 | bytes 209715200 | tf_op jit(solution)/shard_map/dot_general | solution.py:63
  632.7 28.5 convert_reduce_fusion.1
  661.2 10.0 all-to-all-start.1
  671.2 24.6 fusion.11
  701.3 12.0 dynamic-slice_bitcast_fusion
  728.0 845.0 %all-reduce.1 = s32[8]{0:T(128)S(1)} all-reduce(s32[8]{0:T(128)S(1)} %dynamic-update-slice), channel_id=1, replica_groups=mesh['dp'=2,'ep'=8] {'ep'}, use_global_device_ids=true, to_apply=%add.1 | all-reduce | flops 8 | bytes 64
  1578.9 313.1 %select_reduce_fusion = s32[20480]{0:T(1024)S(1)} fusion(s32[20480]{0:T(1024)S(1)} %get-tuple-element.41), kind=kLoop, calls=%fused_computation.5 | loop fusion | flops 1258270720 | bytes 163840 | tf_op jit(solution)/shard_map/reduce_sum | solution.py:34
  1915.4 29.7 collective-permute-done.5
  1948.0 70.6 %pad_maximum_fusion = bf16[20480,2048]{1,0:T(8,128)(2,1)} fusion(bf16[4096,2048]{1,0:T(8,128)(2,1)} %bitcast.119, bf16[16384,2048]{1,0:T(8,128)(2,1)} %bitcast.13), kind=kLoop, calls=%fused_computation.17 | loop fusion | flops 167772160 | bytes 167772160 | tf_op jit(solution)/shard_map/concatenate | solution.py:113
  2018.6 476.8 %gather_fusion.1 = bf16[20480,2048]{1,0:T(8,128)(2,1)} fusion(bf16[20480,2048]{1,0:T(8,128)(2,1)} %pad_maximum_fusion, s32[20480]{0:T(1024)S(1)} %broadcast_clamp_fusion.1), kind=kCustom, calls=%fused_computation.1 | custom fusion | bytes 167854080 | tf_op jit(solution)/shard_map/gather | solution.py:35
  2495.4 123.0 %ragged-dot-none.2 = f32[20480,1024]{1,0:T(8,128)} custom-call(s32[1]{0:T(128)} %get-tuple-element.5, s32[10]{0:T(128)} %get-tuple-element.6, s32[88]{0:T(128)} %get-tuple-element.7, s32[88]{0:T(128)} %get-tuple-element.8, s32[1]{0:T(128)} %get-tuple-element.5, bf16[20480,2048]{1,0:T(8,128)(2,1)} %gather_fusion.1, bf16[9,2048,1024]{2,1,0:T(8,128)(2,1)} %param.11), custom_call_target="tpu_custom_call" | custom-call | flops 85899345920 | bytes 205520928 | tf_op jit(solution)/shard_map/ragged_dot_general/ragged-dot-none
  2618.4 123.0 %ragged-dot-none.1 = f32[20480,1024]{1,0:T(8,128)} custom-call(s32[1]{0:T(128)} %get-tuple-element.5, s32[10]{0:T(128)} %get-tuple-element.6, s32[88]{0:T(128)} %get-tuple-element.7, s32[88]{0:T(128)} %get-tuple-element.8, s32[1]{0:T(128)} %get-tuple-element.5, bf16[20480,2048]{1,0:T(8,128)(2,1)} %gather_fusion.1, bf16[9,2048,1024]{2,1,0:T(8,128)(2,1)} %param.12), custom_call_target="tpu_custom_call" | custom-call | flops 85899345920 | bytes 205520928 | tf_op jit(solution)/shard_map/ragged_dot_general/ragged-dot-none
  2741.4 65.3 %multiply_convert_fusion = bf16[20480,1024]{1,0:T(8,128)(2,1)} fusion(f32[20480,1024]{1,0:T(8,128)} %ragged-dot-none.1, f32[20480,1024]{1,0:T(8,128)} %ragged-dot-none.2), kind=kLoop, calls=%fused_computation.18 | loop fusion | flops 125829120 | bytes 209715200 | tf_op jit(solution)/shard_map/convert_element_type | solution.py:39
  2806.7 119.8 %ragged-dot-none = f32[20480,2048]{1,0:T(8,128)} custom-call(s32[1]{0:T(128)} %get-tuple-element.5, s32[10]{0:T(128)} %get-tuple-element.6, s32[88]{0:T(128)} %get-tuple-element.7, s32[88]{0:T(128)} %get-tuple-element.8, s32[1]{0:T(128)} %get-tuple-element.5, bf16[20480,1024]{1,0:T(8,128)(2,1)} %multiply_convert_fusion, bf16[9,1024,2048]{2,1,0:T(8,128)(2,1)} %param.13), custom_call_target="tpu_custom_call" | custom-call | flops 85899345920 | bytes 247463968 | tf_op jit(solution)/shard_map/ragged_dot_general/ragged-dot-none
  2926.5 79.2 %convert_element_type.96 = bf16[20480,2048]{1,0:T(8,128)(2,1)} convert(f32[20480,2048]{1,0:T(8,128)} %ragged-dot-none) | non-fusion elementwise | flops 41943040 | bytes 251658240 | tf_op jit(solution)/shard_map/convert_element_type | solution.py:40
  3005.7 476.8 %gather_fusion.2 = bf16[20480,2048]{1,0:T(8,128)(2,1)} fusion(bf16[20480,2048]{1,0:T(8,128)(2,1)} %convert_element_type.96, s32[20480]{0:T(1024)S(1)} %copy-done.4), kind=kCustom, calls=%fused_computation.2 | custom fusion | bytes 167854080 | tf_op jit(solution)/shard_map/gather | solution.py:41
  3482.6 55.1 %broadcast_select_fusion = bf16[20480,2048]{1,0:T(8,128)(2,1)} fusion(bf16[20480,2048]{1,0:T(8,128)(2,1)} %gather_fusion.2, pred[20480]{0:T(1024)(128)(4,1)S(1)} %copy-done.6), kind=kLoop, calls=%fused_computation.19 | loop fusion | flops 41943040 | bytes 167792640 | tf_op jit(solution)/shard_map/jit(_where)/select_n | solution.py:41
  3537.7 44.1 slice.84
  3581.7 21.6 all-to-all-start.2
  3603.3 184.6 %fusion.1 = bf16[2048,16384]{1,0:T(8,128)(2,1)} fusion(s32[8,2048]{1,0:T(8,128)S(1)} %copy-done.3, bf16[8,2048]{1,0:T(8,128)(2,1)S(1)} %bitcast.127), kind=kLoop, calls=%fused_computation.12 | loop fusion | flops 771751936 | bytes 67207168 | tf_op jit(solution)/shard_map/reduce_sum | solution.py:74
  3788.0 10.4 fusion.54
  3806.5 8.8 collective-permute-start.9
  3815.3 26.1 fusion.3
  3847.1 522.7 %collective-permute-done.7 = bf16[512,2048]{1,0:T(8,128)(2,1)} collective-permute-done((bf16[512,2048]{1,0:T(8,128)(2,1)}, bf16[512,2048]{1,0:T(8,128)(2,1)}, u32[]{:S(2)}, u32[]{:S(2)}) %collective-permute-start.7) | collective-permute-done | bytes 2097184 | tf_op jit(solution)/shard_map/ppermute | solution.py:119
  4373.0 41.7 collective-permute-done.8
  4419.9 39.7 collective-permute-done.11
  4459.7 44.6 collective-permute-done.12
  4523.7 8.2 pad_maximum_fusion.1
  4531.9 152.9 %fusion.58 = f32[2048,2048]{1,0:T(8,128)} fusion(bf16[2048,16384]{1,0:T(8,128)(2,1)} %fusion.1, bf16[16384,2048]{1,0:T(8,128)(2,1)} %bitcast.49), kind=kOutput, calls=%fused_computation.148 | convolution fusion | flops 137438953472 | bytes 150994944 | tf_op jit(solution)/shard_map/dot_general | solution.py:76
  4684.8 25.4 add_convert_fusion
  (115 shorter events, 106.6 us)
Async XLA Ops:
  10.7 472.1 %copy-start.2 = (s32[8,2048]{1,0:T(8,128)}, s32[8,2048]{1,0:T(8,128)S(1)}, u32[]{:S(2)}) copy-start(s32[8,2048]{1,0:T(8,128)S(1)} %copy.50) | copy-start | bytes 196612
  309.3 351.8 %all-to-all-start = ((s32[8,2048,1]{1,2,0:T(1,128)}), s32[8,2048,1]{1,2,0:T(1,128)}, u32[]{:S(2)}, u32[]{:S(2)}) async-start(s32[8,2048,1]{1,2,0:T(1,128)} %bitcast.5), calls=%async_computation | async-start | bytes 131072 | tf_op jit(solution)/shard_map/all_to_all | solution.py:102
  483.7 149.0 %copy-start = (s32[8,2048]{1,0:T(8,128)S(1)}, s32[8,2048]{1,0:T(8,128)}, u32[]{:S(2)}) copy-start(s32[8,2048]{1,0:T(8,128)} %copy.54) | copy-start | bytes 196612
  661.2 1286.8 %all-to-all-start.1 = ((bf16[8,2048,2048]{2,1,0:T(8,128)(2,1)}), bf16[8,2048,2048]{2,1,0:T(8,128)(2,1)}, u32[]{:S(2)}, u32[]{:S(2)}) async-start(bf16[8,2048,2048]{2,1,0:T(8,128)(2,1)} %bitcast.12), calls=%async_computation.1 | async-start | bytes 134217728 | tf_op jit(solution)/shard_map/all_to_all | solution.py:101
  671.2 24.6 copy-start.7
  701.3 20.7 copy-start.9
  701.3 872.3 %copy-start.8 = (s32[4]{0:T(128)S(1)}, s32[4]{0:T(128)}, u32[]{:S(2)}) copy-start(s32[4]{0:T(128)} %constant.171.clone) | copy-start | bytes 52
  713.3 1183.2 %collective-permute-start = (bf16[512,2048]{1,0:T(8,128)(2,1)}, bf16[512,2048]{1,0:T(8,128)(2,1)}, u32[]{:S(2)}, u32[]{:S(2)}) collective-permute-start(bf16[512,2048]{1,0:T(8,128)(2,1)} %get-tuple-element.34), channel_id=1, source_target_pairs={{0,1},{3,4},{4,5},{7,0},{8,9},{11,12},{12,13},{15,8}} | collective-permute-start | bytes 6291464 | tf_op jit(solution)/shard_map/ppermute | solution.py:107
  715.7 1185.3 %collective-permute-start.1 = (bf16[512,2048]{1,0:T(8,128)(2,1)}, bf16[512,2048]{1,0:T(8,128)(2,1)}, u32[]{:S(2)}, u32[]{:S(2)}) collective-permute-start(bf16[512,2048]{1,0:T(8,128)(2,1)} %get-tuple-element.33), channel_id=1, source_target_pairs={{2,4},{3,5},{6,0},{7,1},{10,12},{11,13},{14,8},{15,9}} | collective-permute-start | bytes 6291464 | tf_op jit(solution)/shard_map/ppermute | solution.py:107
  717.0 1188.9 %collective-permute-start.2 = (bf16[512,2048]{1,0:T(8,128)(2,1)}, bf16[512,2048]{1,0:T(8,128)(2,1)}, u32[]{:S(2)}, u32[]{:S(2)}) collective-permute-start(bf16[512,2048]{1,0:T(8,128)(2,1)} %get-tuple-element.32), channel_id=1, source_target_pairs={{1,4},{2,5},{5,0},{6,1},{9,12},{10,13},{13,8},{14,9}} | collective-permute-start | bytes 6291464 | tf_op jit(solution)/shard_map/ppermute | solution.py:107
  718.3 1190.7 %collective-permute-start.3 = (bf16[512,2048]{1,0:T(8,128)(2,1)}, bf16[512,2048]{1,0:T(8,128)(2,1)}, u32[]{:S(2)}, u32[]{:S(2)}) collective-permute-start(bf16[512,2048]{1,0:T(8,128)(2,1)} %get-tuple-element.31), channel_id=1, source_target_pairs={{0,4},{1,5},{4,0},{5,1},{8,12},{9,13},{12,8},{13,9}} | collective-permute-start | bytes 6291464 | tf_op jit(solution)/shard_map/ppermute | solution.py:107
  724.0 1188.2 %collective-permute-start.4 = (bf16[512,2048]{1,0:T(8,128)(2,1)}, bf16[512,2048]{1,0:T(8,128)(2,1)}, u32[]{:S(2)}, u32[]{:S(2)}) collective-permute-start(bf16[512,2048]{1,0:T(8,128)(2,1)} %get-tuple-element.30), channel_id=1, source_target_pairs={{0,5},{3,0},{4,1},{7,4},{8,13},{11,8},{12,9},{15,12}} | collective-permute-start | bytes 6291464 | tf_op jit(solution)/shard_map/ppermute | solution.py:107
  1896.5 48.5 %collective-permute-start.5 = (bf16[512,2048]{1,0:T(8,128)(2,1)}, bf16[512,2048]{1,0:T(8,128)(2,1)S(1)}, u32[]{:S(2)}, u32[]{:S(2)}) collective-permute-start(bf16[512,2048]{1,0:T(8,128)(2,1)} %get-tuple-element.29), channel_id=1, source_target_pairs={{2,0},{3,1},{6,4},{7,5},{10,8},{11,9},{14,12},{15,13}} | collective-permute-start | bytes 6291464 | tf_op jit(solution)/shard_map/ppermute | solution.py:107
  1901.0 45.6 collective-permute-start.6
  2926.5 79.2 %copy-start.4 = (s32[20480]{0:T(1024)S(1)}, s32[20480]{0:T(1024)}, u32[]{:S(2)}) copy-start(s32[20480]{0:T(1024)} %broadcast_clamp_fusion) | copy-start | bytes 245764
  3005.7 476.8 %copy-start.6 = (pred[20480]{0:T(1024)(128)(4,1)S(1)}, pred[20480]{0:T(1024)(128)(4,1)}, u32[]{:S(2)}) copy-start(pred[20480]{0:T(1024)(128)(4,1)} %fusion.43) | copy-start | bytes 61444
  3581.7 21.6 copy-start.3
  3581.7 21.6 copy-start.5
  3581.7 950.1 %all-to-all-start.2 = ((bf16[8,2048,2048]{2,1,0:T(8,128)(2,1)}), bf16[8,2048,2048]{2,1,0:T(8,128)(2,1)}, u32[]{:S(2)}, u32[]{:S(2)}) async-start(bf16[8,2048,2048]{2,1,0:T(8,128)(2,1)} %bitcast.48), calls=%async_computation.2 | async-start | bytes 134217728 | tf_op jit(solution)/shard_map/all_to_all | solution.py:114
  3788.0 27.3 copy-start.1
  3798.4 571.3 %collective-permute-start.7 = (bf16[512,2048]{1,0:T(8,128)(2,1)}, bf16[512,2048]{1,0:T(8,128)(2,1)}, u32[]{:S(2)}, u32[]{:S(2)}) collective-permute-start(bf16[512,2048]{1,0:T(8,128)(2,1)} %get-tuple-element.25), channel_id=1, source_target_pairs={{1,0},{4,3},{5,4},{0,7},{9,8},{12,11},{13,12},{8,15}} | collective-permute-start | bytes 6291464 | tf_op jit(solution)/shard_map/ppermute | solution.py:119
  3803.0 611.7 %collective-permute-start.8 = (bf16[512,2048]{1,0:T(8,128)(2,1)}, bf16[512,2048]{1,0:T(8,128)(2,1)}, u32[]{:S(2)}, u32[]{:S(2)}) collective-permute-start(bf16[512,2048]{1,0:T(8,128)(2,1)} %get-tuple-element.24), channel_id=1, source_target_pairs={{4,2},{5,3},{0,6},{1,7},{12,10},{13,11},{8,14},{9,15}} | collective-permute-start | bytes 6291464 | tf_op jit(solution)/shard_map/ppermute | solution.py:119
  3806.5 611.4 %collective-permute-start.9 = (bf16[512,2048]{1,0:T(8,128)(2,1)}, bf16[512,2048]{1,0:T(8,128)(2,1)}, u32[]{:S(2)}, u32[]{:S(2)}) collective-permute-start(bf16[512,2048]{1,0:T(8,128)(2,1)} %get-tuple-element.23), channel_id=1, source_target_pairs={{4,1},{5,2},{0,5},{1,6},{12,9},{13,10},{8,13},{9,14}} | collective-permute-start | bytes 6291464 | tf_op jit(solution)/shard_map/ppermute | solution.py:119
  3841.4 578.4 %collective-permute-start.10 = (bf16[512,2048]{1,0:T(8,128)(2,1)}, bf16[512,2048]{1,0:T(8,128)(2,1)S(1)}, u32[]{:S(2)}, u32[]{:S(2)}) collective-permute-start(bf16[512,2048]{1,0:T(8,128)(2,1)} %get-tuple-element.22), channel_id=1, source_target_pairs={{4,0},{5,1},{0,4},{1,5},{12,8},{13,9},{8,12},{9,13}} | collective-permute-start | bytes 6291464 | tf_op jit(solution)/shard_map/ppermute | solution.py:119
  3843.3 616.3 %collective-permute-start.11 = (bf16[512,2048]{1,0:T(8,128)(2,1)}, bf16[512,2048]{1,0:T(8,128)(2,1)S(1)}, u32[]{:S(2)}, u32[]{:S(2)}) collective-permute-start(bf16[512,2048]{1,0:T(8,128)(2,1)} %get-tuple-element.21), channel_id=1, source_target_pairs={{5,0},{0,3},{1,4},{4,7},{13,8},{8,11},{9,12},{12,15}} | collective-permute-start | bytes 6291464 | tf_op jit(solution)/shard_map/ppermute | solution.py:119
  4369.7 134.7 %collective-permute-start.12 = (bf16[512,2048]{1,0:T(8,128)(2,1)}, bf16[512,2048]{1,0:T(8,128)(2,1)S(1)}, u32[]{:S(2)}, u32[]{:S(2)}) collective-permute-start(bf16[512,2048]{1,0:T(8,128)(2,1)} %get-tuple-element.20), channel_id=1, source_target_pairs={{0,2},{1,3},{4,6},{5,7},{8,10},{9,11},{12,14},{13,15}} | collective-permute-start | bytes 6291464 | tf_op jit(solution)/shard_map/ppermute | solution.py:119
  4414.7 89.9 %collective-permute-start.13 = (bf16[512,2048]{1,0:T(8,128)(2,1)S(1)}, bf16[512,2048]{1,0:T(8,128)(2,1)S(1)}, u32[]{:S(2)}, u32[]{:S(2)}) collective-permute-start(bf16[512,2048]{1,0:T(8,128)(2,1)S(1)} %get-tuple-element.19), channel_id=1, source_target_pairs={{0,1},{1,2},{4,5},{5,6},{8,9},{9,10},{12,13},{13,14}} | collective-permute-start | bytes 6291464 | tf_op jit(solution)/shard_map/ppermute | solution.py:119
where the time goes:
time: 4750 us; the launch traced here: 4710 us
  other arithmetic  1310 us (28%)
  local copies, waits for them, and re-layouts  1080 us (23%)
  blocking collectives  845 us (18%)
  waiting for transfers between devices  678 us (14%)
  Pallas kernels  368 us (8%)
  matrix products  352 us (7%)
  starting transfers between devices  76.4 us (2%)
    unnamed x1, blocking collectives  845 us
    ppermute x7, waiting for transfers between devices, local(): back.append(lax.ppermute(hout[dl], 'ep', pairs))  649 us
    gather x1, local copies, waits for them, and re-layouts, grouped_ffn(): return jnp.where((gid < g)[:, None], o[pos], jnp.zeros((), jnp.bfloat16))  477 us
    gather x1, local copies, waits for them, and re-layouts, grouped_ffn(): xs = rows[perm]  477 us
    another operation x3, Pallas kernels  366 us
    reduce_sum x1, other arithmetic, grouped_ffn(): perm = jnp.sum(jnp.where(pos[:, None] == q[None, :], q[:, None], 0), axis=0)  313 us
    reduce_sum x1, other arithmetic, pack(): jnp.sum(jnp.where(cm, value_a5 - lslot.reshape(td, k).T[:, None, :], 0),...  298 us
    reduce_sum x1, other arithmetic, combine(): jnp.sum(jnp.where(cpos.reshape(td, k).T[:, :, None] == jnp.arange(cret.sh...  185 us
  transfers between devices with their start and end apart: 17, of which 5 were waited for; matrix products, arithmetic and copies ran while one was open for 21% of the time, Pallas kernels for 0%

commit v1 on v0

v1 whole, which is shorter than its diff:
```python
import functools

import jax
import jax.numpy as jnp
from jax import lax
from jax.experimental import pallas as pl
from jax.experimental.pallas import tpu as pltpu
from jax.sharding import PartitionSpec as P

CHUNKS = 4
GR = 16
GB = 16
BR = GR * GB
WT = 512
SP = 16


def holder_list(p):
    return [0, (p // 2 + 1) % p, (p // 4 + 2) % p, (3 * p // 4 + 3) % p]


def pack_kernel(wid, nblk, pos_ref, x_ref, o_ref, *, slots):
    j = pl.program_id(0)

    @pl.when(j < nblk[0])
    def _():
        pack_block(j, pos_ref, x_ref, o_ref, slots)


def pack_block(j, pos_ref, x_ref, o_ref, slots):
    rows = lax.broadcasted_iota(jnp.int32, (BR, WT), 0) + j * BR
    oh = pos_ref[0:1, :] == rows
    for s in range(1, slots):
        oh = jnp.logical_or(oh, pos_ref[s:s + 1, :] == rows)
    oh = jnp.where(oh, 1.0, 0.0).astype(jnp.bfloat16)
    d = x_ref.shape[1]
    step = 512
    for n in range(0, d, step):
        r = jnp.dot(oh, x_ref[:, n:n + step], preferred_element_type=jnp.float32)
        o_ref[:, :, n:n + step] = r.astype(jnp.bfloat16).reshape(GB, GR, step)


def pack(wid, nblk, pos, x, ng, slots):
    d = x.shape[1]
    return pl.pallas_call(
        functools.partial(pack_kernel, slots=slots),
        grid_spec=pltpu.PrefetchScalarGridSpec(
            num_scalar_prefetch=2,
            grid=wid.shape,
            in_specs=[
                pl.BlockSpec((SP, WT), lambda j, wid, nb: (0, wid[j])),
                pl.BlockSpec((WT, d), lambda j, wid, nb: (wid[j], 0)),
            ],
            out_specs=pl.BlockSpec((GB, GR, d), lambda j, wid, nb: (jnp.minimum(j, nb[0] - 1), 0, 0)),
        ),
        out_shape=jax.ShapeDtypeStruct((ng, GR, d), jnp.bfloat16),
        cost_estimate=pl.CostEstimate(flops=2 * 24 * BR * WT * d, bytes_accessed=24 * BR * d * 4, transcendentals=0),
        name="pack",
    )(wid, nblk, pos, x)


def ffn_kernel(bexp, grp, nb, xs, w1, w3, w2, o, xbuf, obuf, abuf, isem, osem):
    i = pl.program_id(0)
    n = nb[0]

    @pl.when(i < n)
    def _():
        ffn_block(i, n, grp, xs, w1, w3, w2, o, xbuf, obuf, abuf, isem, osem)


def ffn_block(i, n, grp, xs, w1, w3, w2, o, xbuf, obuf, abuf, isem, osem):
    slot = lax.rem(i, 2)

    def start_in(b, sl):
        for g in range(GB):
            pltpu.make_async_copy(xs.at[grp[b * GB + g]], xbuf.at[sl, g], isem.at[sl]).start()

    @pl.when(i == 0)
    def _():
        start_in(0, 0)

    @pl.when(i + 1 < n)
    def _():
        start_in(i + 1, 1 - slot)

    pltpu.make_async_copy(xs.at[pl.ds(0, GB)], xbuf.at[slot], isem.at[slot]).wait()

    @pl.when(i >= 2)
    def _():
        pltpu.make_async_copy(obuf.at[slot], o.at[pl.ds(0, GB)], osem.at[slot]).wait()

    d = xs.shape[2]
    ff = w1.shape[2]
    x = xbuf[slot].reshape(BR, d)
    step = 256
    for c in range(0, ff, step):
        u = jnp.dot(x, w1[0, :, c:c + step], preferred_element_type=jnp.float32)
        v = jnp.dot(x, w3[0, :, c:c + step], preferred_element_type=jnp.float32)
        abuf[:, c:c + step] = (jax.nn.silu(u) * v).astype(jnp.bfloat16)
    a = abuf[...]
    step = 512
    for c in range(0, d, step):
        r = jnp.dot(a, w2[0, :, c:c + step], preferred_element_type=jnp.float32)
        obuf[slot, :, :, c:c + step] = r.astype(jnp.bfloat16).reshape(GB, GR, step)

    for g in range(GB):
        pltpu.make_async_copy(obuf.at[slot, g], o.at[grp[i * GB + g]], osem.at[slot]).start()

    @pl.when(i == n - 1)
    def _():
        pltpu.make_async_copy(obuf.at[slot], o.at[pl.ds(0, GB)], osem.at[slot]).wait()

        @pl.when(i >= 1)
        def _():
            pltpu.make_async_copy(obuf.at[1 - slot], o.at[pl.ds(0, GB)], osem.at[1 - slot]).wait()


def ffn(bexp, grp, nb, xs, w1, w3, w2):
    ng, _, d = xs.shape
    ff = w1.shape[2]
    return pl.pallas_call(
        ffn_kernel,
        grid_spec=pltpu.PrefetchScalarGridSpec(
            num_scalar_prefetch=3,
            grid=bexp.shape,
            in_specs=[
                pl.BlockSpec(memory_space=pl.ANY),
                pl.BlockSpec((1, d, ff), lambda i, be, gr, nb: (be[i], 0, 0)),
                pl.BlockSpec((1, d, ff), lambda i, be, gr, nb: (be[i], 0, 0)),
                pl.BlockSpec((1, ff, d), lambda i, be, gr, nb: (be[i], 0, 0)),
            ],
            out_specs=pl.BlockSpec(memory_space=pl.ANY),
            scratch_shapes=[
                pltpu.VMEM((2, GB, GR, d), jnp.bfloat16),
                pltpu.VMEM((2, GB, GR, d), jnp.bfloat16),
                pltpu.VMEM((BR, ff), jnp.bfloat16),
                pltpu.SemaphoreType.DMA((2,)),
                pltpu.SemaphoreType.DMA((2,)),
            ],
        ),
        out_shape=jax.ShapeDtypeStruct((ng, GR, d), jnp.bfloat16),
        compiler_params=pltpu.CompilerParams(vmem_limit_bytes=56 * 2 ** 20),
        cost_estimate=pl.CostEstimate(flops=6 * 24 * BR * d * ff, bytes_accessed=24 * BR * d * 4, transcendentals=0),
        name="ffn",
    )(bexp, grp, nb, xs, w1, w3, w2)


def combine_kernel(wid, first, nval, nblk, pos_ref, gate_ref, o_ref, y_ref, *, slots):
    j = pl.program_id(0)

    @pl.when(j < nblk[0])
    def _():
        combine_block(j, first, nval, pos_ref, gate_ref, o_ref, y_ref, slots)


def combine_block(j, first, nval, pos_ref, gate_ref, o_ref, y_ref, slots):
    rows = lax.broadcasted_iota(jnp.int32, (BR, WT), 0) + j * BR
    gm = jnp.zeros((BR, WT), jnp.float32)
    for s in range(slots):
        gm = jnp.where(pos_ref[s:s + 1, :] == rows, gate_ref[s:s + 1, :], gm)
    gm = gm.astype(jnp.bfloat16)
    d = y_ref.shape[1]
    step = 512
    live = lax.broadcasted_iota(jnp.int32, (BR, step), 0) < nval[j]
    for c in range(0, d, step):
        o = o_ref[:, :, c:c + step].reshape(BR, step)
        o = jnp.where(live, o, jnp.zeros((), jnp.bfloat16))
        r = lax.dot_general(gm, o, (((0,), (0,)), ((), ())), preferred_element_type=jnp.float32)

        @pl.when(first[j] == 1)
        def _():
            y_ref[:, c:c + step] = r

        @pl.when(first[j] == 0)
        def _():
            y_ref[:, c:c + step] += r


def combine(wid, first, nval, nblk, pos, gate, o, slots):
    d = o.shape[2]
    t = pos.shape[1]
    return pl.pallas_call(
        functools.partial(combine_kernel, slots=slots),
        grid_spec=pltpu.PrefetchScalarGridSpec(
            num_scalar_prefetch=4,
            grid=wid.shape,
            in_specs=[
                pl.BlockSpec((SP, WT), lambda j, wid, f, v, nb: (0, wid[j])),
                pl.BlockSpec((SP, WT), lambda j, wid, f, v, nb: (0, wid[j])),
                pl.BlockSpec((GB, GR, d), lambda j, wid, f, v, nb: (jnp.minimum(j, nb[0] - 1), 0, 0)),
            ],
            out_specs=pl.BlockSpec((WT, d), lambda j, wid, f, v, nb: (wid[j], 0)),
        ),
        out_shape=jax.ShapeDtypeStruct((t, d), jnp.float32),
        cost_estimate=pl.CostEstimate(flops=2 * 24 * BR * WT * d, bytes_accessed=24 * BR * d * 8, transcendentals=0),
        name="combine",
    )(wid, first, nval, nblk, pos, gate, o)


def solution(mesh):
    p = mesh.shape["ep"]
    hold = holder_list(p)
    nh = len(hold)
    table = [hold.index(q) if q in hold else nh for q in range(p)]

    def local(x, ridx, gates, w1, w3, w2):
        td, d = x.shape
        k = ridx.shape[1]
        slots = w1.shape[0]
        loc = slots - 1
        nc = CHUNKS
        tc = td // nc
        tch = tc * p
        nw = tch // WT
        me = lax.axis_index("ep")
        gme = jnp.array(table, jnp.int32)[me]

        rmax = p * min(td * k // p, tc * k) + -(-tch // nh)
        gmax = rmax // GR + nw * slots
        wbmax = gmax // GB + nw
        ebmax = gmax // GB + slots
        ng = (wbmax + 2) * GB
        trash = wbmax * GB

        def chunked(v):
            a = lax.all_gather(v.T, "ep", axis=1, tiled=False)
            return a.reshape(k, p, nc, tc).transpose(0, 2, 1, 3).reshape(k, nc * tch)
        rt = chunked(ridx)
        gt = chunked(gates).astype(jnp.float32)
        s_id = jnp.arange(slots, dtype=jnp.int32)
        eid = jnp.where(s_id < loc, me * loc + s_id, jnp.where(jnp.logical_and(gme < nh, me != 0), 0, -1))
        share = jnp.arange(nc * tch, dtype=jnp.int32) % nh == gme
        match = rt[:, None, :] == eid[None, :, None]
        match = jnp.logical_and(match, jnp.logical_or(eid[None, :, None] != 0, share[None, None, :]))
        sel = jnp.any(match, axis=0)
        gate = jnp.sum(jnp.where(match, gt[:, None, :], 0.0), axis=0)
        selb = sel.astype(jnp.bfloat16).reshape(slots * nc * nw, WT)
        tri = (jnp.arange(WT)[:, None] < jnp.arange(WT)[None, :]).astype(jnp.bfloat16)
        rank = jnp.dot(selb, tri, preferred_element_type=jnp.float32).astype(jnp.int32)
        rank = rank.reshape(slots, nc, nw, WT)
        selw = sel.reshape(slots, nc, nw, WT)
        cnt = rank[..., -1] + selw[..., -1].astype(jnp.int32)
        n_g = ((cnt + GR - 1) // GR).transpose(1, 2, 0)
        g_off = jnp.cumsum(n_g, axis=2) - n_g
        g_w = jnp.sum(n_g, axis=2)
        nb_w = jnp.maximum((g_w + GB - 1) // GB, 1)
        b_end = jnp.cumsum(nb_w, axis=1)
        b_off = b_end - nb_w
        base = b_off[:, :, None] * GB + g_off
        pos = jnp.where(selw, base.transpose(2, 0, 1)[..., None] * GR + rank, -1).reshape(slots, nc, tch)
        pos = jnp.pad(pos, ((0, SP - slots), (0, 0), (0, 0)), constant_values=-1)
        gate = jnp.pad(gate.reshape(slots, nc, tch), ((0, SP - slots), (0, 0), (0, 0)))

        jb = jnp.arange(wbmax, dtype=jnp.int32)
        wid = jnp.minimum(jnp.sum((jb[None, :, None] >= b_end[:, None, :]).astype(jnp.int32), axis=2), nw - 1)
        ohw = wid[:, :, None] == jnp.arange(nw)
        jrel = jb[None, :] - jnp.sum(jnp.where(ohw, b_off[:, None, :], 0), axis=2)
        nval = jnp.clip(jnp.sum(jnp.where(ohw, g_w[:, None, :], 0), axis=2) * GR - jrel * BR, 0, BR)
        first = (jrel == 0).astype(jnp.int32)
        nblk = b_end[:, -1:]

        w_end = jnp.cumsum(n_g, axis=1)
        tg = w_end[:, -1, :]
        nb_s = (tg + GB - 1) // GB
        e_end = jnp.cumsum(nb_s, axis=1)
        ib = jnp.arange(ebmax, dtype=jnp.int32)
        bexp = jnp.minimum(jnp.sum((ib[None, :, None] >= e_end[:, None, :]).astype(jnp.int32), axis=2), slots - 1)
        ohs = bexp[:, :, None] == s_id
        irel = ib[None, :] - jnp.sum(jnp.where(ohs, (e_end - nb_s)[:, None, :], 0), axis=2)
        q = irel[:, :, None] * GB + jnp.arange(GB, dtype=jnp.int32)
        pick = lambda v: jnp.sum(jnp.where(ohs[:, :, None, :], v[:, None, :, :], 0), axis=3)
        we, wn, wbase = pick(w_end), pick(n_g), pick(base)
        ws = we - wn
        hit = jnp.logical_and(q[..., None] >= ws[:, :, None, :], q[..., None] < we[:, :, None, :])
        src = jnp.sum(jnp.where(hit, (wbase - ws)[:, :, None, :] + q[..., None], 0), axis=3)
        spare = trash + (ib[:, None] % 2) * GB + jnp.arange(GB, dtype=jnp.int32)[None, :]
        grp = jnp.where(jnp.any(hit, axis=3), src, spare[None]).reshape(nc, ebmax * GB)
        nb = jnp.maximum(e_end[:, -1:], 1)

        ys = []
        for c in range(nc):
            xa = lax.all_gather(x[c * tc:(c + 1) * tc], "ep", axis=0, tiled=True)
            xs = pack(wid[c], nblk[c], pos[:, c], xa, ng, slots)
            o = ffn(bexp[c], grp[c], nb[c], xs, w1, w3, w2)
            yp = combine(wid[c], first[c], nval[c], nblk[c], pos[:, c], gate[:, c], o, slots)
            ys.append(lax.psum_scatter(yp, "ep", scatter_dimension=0, tiled=True).astype(jnp.bfloat16))
        return jnp.concatenate(ys, axis=0)

    spec_t = P(("dp", "ep"), None)
    spec_w = P("ep", None, None)
    return jax.shard_map(local, mesh=mesh, in_specs=(spec_t, spec_t, spec_t, spec_w, spec_w, spec_w), out_specs=spec_t, check_vma=False)
```

time: 4750 us -> 1200 us (0.25)
  other arithmetic: 1310 us -> 27.1 us
  local copies, waits for them, and re-layouts: 1080 us -> 21.6 us
  blocking collectives: 845 us -> 23.4 us
  Pallas kernels: 368 us -> 758 us
  matrix products: 352 us -> 0.33 us
  waiting for transfers between devices: 678 us -> 345 us
  starting transfers between devices: 76.4 us -> 0.75 us
    reduce_sum x8, other arithmetic: 1020 us -> 3.01 us  [the longest x1 2.21 us: local(): gate = jnp.sum(jnp.where(match, gt[:, None, :], 0.0), axis=0)]
    gather x6 -> x0, local copies, waits for them, and re-layouts: 973 us -> none  [the longest x1 477 us: grouped_ffn(): return jnp.where((gid < g)[:, None], o[pos], jnp.zeros((), jnp.bfloat16))]
    unnamed x1 -> x0, blocking collectives: 845 us -> none
    pallas_call x0 -> x12, Pallas kernels: none -> 758 us  [the longest x4 401 us: ffn(): pl.pallas_call(ffn_kernel, grid_spec=pltpu.PrefetchScalarGridSpec(num_sca...]
    ppermute x14 -> x0, waiting for transfers between devices: 678 us -> none  [the longest x7 649 us: local(): back.append(lax.ppermute(hout[dl], 'ep', pairs))]
    another operation x3 -> x0, Pallas kernels: 366 us -> none
    dot_general x6 -> x1, matrix products: 352 us -> 0.33 us  [local(): jnp.dot(selb, tri, preferred_element_type=jnp.float32).astype(jnp.int32)]
    reduce_scatter x0 -> x4, waiting for transfers between devices: none -> 300 us  [local(): lax.psum_scatter(yp, 'ep', scatter_dimension=0, tiled=True)]
  transfers between devices with their start and end apart: 17 -> 8, of which waited for: 5 -> 3; matrix products, arithmetic and copies ran while one was open for 21% -> 3% of each run, Pallas kernels for 0% -> 64%
where the time goes in v1:
time: 1200 us; the launch traced here: 1190 us
  Pallas kernels  758 us (63%)
  waiting for transfers between devices  345 us (29%)
  other arithmetic  27.1 us (2%)
  blocking collectives  23.4 us (2%)
  local copies, waits for them, and re-layouts  21.6 us (2%)
  between operations  15 us (1%)
    pallas_call x4, Pallas kernels, ffn(): pl.pallas_call(ffn_kernel, grid_spec=pltpu.PrefetchScalarGridSpec(num_sca...  401 us
    reduce_scatter x4, waiting for transfers between devices, local(): lax.psum_scatter(yp, 'ep', scatter_dimension=0, tiled=True)  300 us
    pallas_call x4, Pallas kernels, combine(): pl.pallas_call(functools.partial(combine_kernel, slots=slots), grid_spec=...  205 us
    pallas_call x4, Pallas kernels, pack(): pl.pallas_call(functools.partial(pack_kernel, slots=slots), grid_spec=plt...  153 us
    all_gather x4, waiting for transfers between devices, local(): xa = lax.all_gather(x[c * tc:(c + 1) * tc], 'ep', axis=0, tiled=True)  42.9 us
  transfers between devices with their start and end apart: 8, of which 3 were waited for; matrix products, arithmetic and copies ran while one was open for 3% of the time, Pallas kernels for 64%

profile of v1, /device:TPU:0, one launch (start us, length us, event | category | flops | bytes accessed | tf_op | source)
XLA Modules:
  0.0 1191.2 jit_solution(18182641829568405399)
XLA Ops:
  6.5 6.0 fusion.30
  12.6 0.7 all-gather.9.cloned.1.call-update
  14.7 11.6 all-gather
  29.0 2.1 fusion
  38.0 11.8 all-gather.1
  50.3 2.2 select_reduce_fusion
  56.7 0.8 fusion.1
  57.5 1.1 fusion.2
  58.6 1.0 fusion.6
  59.6 42.9 %all-gather.7.cloned.1.call-done.x_ref = bf16[4096,2048]{1,0:T(8,128)(2,1)} async-done(((bf16[512,2048]{1,0:T(8,128)(2,1)}), bf16[4096,2048]{1,0:T(8,128)(2,1)}) %all-gather.7.cloned.1.call-update) | async-done | bytes 16777232 | tf_op jit(solution)/shard_map/all_gather | solution.py:282
  102.5 38.2 %pack.4.xs = bf16[1312,16,2048]{2,1,0:T(8,128)(2,1)} custom-call(s32[80]{0:T(128)} %get-tuple-element.52.wid, s32[1]{0:T(128)} %bitcast.10.nblk, s32[16,4096]{1,0:T(8,128)} %get-tuple-element.24.pos_ref, bf16[4096,2048]{1,0:T(8,128)(2,1)} %all-gather.7.cloned.1.call-done.x_ref), custom_call_target="tpu_custom_call" | custom-call | flops 12884901888 | bytes 50331648 | tf_op jit(solution)/shard_map/pack/pallas_call | solution.py:45
  140.7 100.1 %ffn.4.o_ref = bf16[1312,16,2048]{2,1,0:T(8,128)(2,1)} custom-call(s32[81]{0:T(128)} %get-tuple-element.36.bexp, s32[1296]{0:T(1024)} %squeeze.134.grp, s32[1]{0:T(128)} %bitcast.22.nb, bf16[1312,16,2048]{2,1,0:T(8,128)(2,1)} %pack.4.xs, bf16[9,2048,1024]{2,1,0:T(8,128)(2,1)} %w1.7, bf16[9,2048,1024]{2,1,0:T(8,128)(2,1)} %w3.7, bf16[9,1024,2048]{2,1,0:T(8,128)(2,1)} %w2.7), custom_call_target="tpu_custom_call" | custom-call | flops 77309411328 | bytes 50331648 | tf_op jit(solution)/shard_map/ffn/pallas_call | solution.py:121
  240.8 51.2 %combine.4 = f32[4096,2048]{1,0:T(8,128)} custom-call(s32[80]{0:T(128)} %get-tuple-element.52.wid, s32[80]{0:T(128)} %get-tuple-element.59.first, s32[80]{0:T(128)} %get-tuple-element.44.nval, s32[1]{0:T(128)} %bitcast.10.nblk, s32[16,4096]{1,0:T(8,128)} %get-tuple-element.24.pos_ref, f32[16,4096]{1,0:T(8,128)} %get-tuple-element.20.gate_ref, ...), custom_call_target="tpu_custom_call" | custom-call | flops 12884901888 | bytes 100663296 | tf_op jit(solution)/shard_map/combine/pallas_call | solution.py:182
  292.9 0.7 squeeze.143.grp
  293.5 38.1 %pack.5.xs = bf16[1312,16,2048]{2,1,0:T(8,128)(2,1)} custom-call(s32[80]{0:T(128)} %get-tuple-element.55.wid, s32[1]{0:T(128)} %bitcast.26.nblk, s32[16,4096]{1,0:T(8,128)} %get-tuple-element.25.pos_ref, bf16[4096,2048]{1,0:T(8,128)(2,1)} %all-gather.9.cloned.1.call-done.x_ref), custom_call_target="tpu_custom_call" | custom-call | flops 12884901888 | bytes 50331648 | tf_op jit(solution)/shard_map/pack/pallas_call | solution.py:45
  331.7 100.1 %ffn.5.o_ref = bf16[1312,16,2048]{2,1,0:T(8,128)(2,1)} custom-call(s32[81]{0:T(128)} %get-tuple-element.39.bexp, s32[1296]{0:T(1024)} %squeeze.143.grp, s32[1]{0:T(128)} %bitcast.30.nb, bf16[1312,16,2048]{2,1,0:T(8,128)(2,1)} %pack.5.xs, bf16[9,2048,1024]{2,1,0:T(8,128)(2,1)} %w1.7, bf16[9,2048,1024]{2,1,0:T(8,128)(2,1)} %w3.7, bf16[9,1024,2048]{2,1,0:T(8,128)(2,1)} %w2.7), custom_call_target="tpu_custom_call" | custom-call | flops 77309411328 | bytes 50331648 | tf_op jit(solution)/shard_map/ffn/pallas_call | solution.py:121
  431.8 51.2 %combine.5 = f32[4096,2048]{1,0:T(8,128)} custom-call(s32[80]{0:T(128)} %get-tuple-element.55.wid, s32[80]{0:T(128)} %get-tuple-element.56.first, s32[80]{0:T(128)} %get-tuple-element.47.nval, s32[1]{0:T(128)} %bitcast.26.nblk, s32[16,4096]{1,0:T(8,128)} %get-tuple-element.25.pos_ref, f32[16,4096]{1,0:T(8,128)} %get-tuple-element.21.gate_ref, ...), custom_call_target="tpu_custom_call" | custom-call | flops 12884901888 | bytes 100663296 | tf_op jit(solution)/shard_map/combine/pallas_call | solution.py:182
  483.8 0.7 squeeze.152.grp
  484.4 38.1 %pack.6.xs = bf16[1312,16,2048]{2,1,0:T(8,128)(2,1)} custom-call(s32[80]{0:T(128)} %get-tuple-element.54.wid, s32[1]{0:T(128)} %bitcast.34.nblk, s32[16,4096]{1,0:T(8,128)} %get-tuple-element.26.pos_ref, bf16[4096,2048]{1,0:T(8,128)(2,1)} %all-gather.11.cloned.1.call-done.x_ref), custom_call_target="tpu_custom_call" | custom-call | flops 12884901888 | bytes 50331648 | tf_op jit(solution)/shard_map/pack/pallas_call | solution.py:45
  522.6 100.2 %ffn.6.o_ref = bf16[1312,16,2048]{2,1,0:T(8,128)(2,1)} custom-call(s32[81]{0:T(128)} %get-tuple-element.38.bexp, s32[1296]{0:T(1024)} %squeeze.152.grp, s32[1]{0:T(128)} %bitcast.38.nb, bf16[1312,16,2048]{2,1,0:T(8,128)(2,1)} %pack.6.xs, bf16[9,2048,1024]{2,1,0:T(8,128)(2,1)} %w1.7, bf16[9,2048,1024]{2,1,0:T(8,128)(2,1)} %w3.7, bf16[9,1024,2048]{2,1,0:T(8,128)(2,1)} %w2.7), custom_call_target="tpu_custom_call" | custom-call | flops 77309411328 | bytes 50331648 | tf_op jit(solution)/shard_map/ffn/pallas_call | solution.py:121
  622.7 51.1 %combine.6 = f32[4096,2048]{1,0:T(8,128)} custom-call(s32[80]{0:T(128)} %get-tuple-element.54.wid, s32[80]{0:T(128)} %get-tuple-element.57.first, s32[80]{0:T(128)} %get-tuple-element.46.nval, s32[1]{0:T(128)} %bitcast.34.nblk, s32[16,4096]{1,0:T(8,128)} %get-tuple-element.26.pos_ref, f32[16,4096]{1,0:T(8,128)} %get-tuple-element.22.gate_ref, ...), custom_call_target="tpu_custom_call" | custom-call | flops 12884901888 | bytes 100663296 | tf_op jit(solution)/shard_map/combine/pallas_call | solution.py:182
  674.7 0.7 squeeze.161.grp
  675.3 38.1 %pack.7.xs = bf16[1312,16,2048]{2,1,0:T(8,128)(2,1)} custom-call(s32[80]{0:T(128)} %get-tuple-element.53.wid, s32[1]{0:T(128)} %bitcast.42.nblk, s32[16,4096]{1,0:T(8,128)} %get-tuple-element.27.pos_ref, bf16[4096,2048]{1,0:T(8,128)(2,1)} %all-gather.13.cloned.1.call-done.x_ref), custom_call_target="tpu_custom_call" | custom-call | flops 12884901888 | bytes 50331648 | tf_op jit(solution)/shard_map/pack/pallas_call | solution.py:45
  713.4 100.2 %ffn.7.o_ref = bf16[1312,16,2048]{2,1,0:T(8,128)(2,1)} custom-call(s32[81]{0:T(128)} %get-tuple-element.37.bexp, s32[1296]{0:T(1024)} %squeeze.161.grp, s32[1]{0:T(128)} %bitcast.46.nb, bf16[1312,16,2048]{2,1,0:T(8,128)(2,1)} %pack.7.xs, bf16[9,2048,1024]{2,1,0:T(8,128)(2,1)} %w1.7, bf16[9,2048,1024]{2,1,0:T(8,128)(2,1)} %w3.7, bf16[9,1024,2048]{2,1,0:T(8,128)(2,1)} %w2.7), custom_call_target="tpu_custom_call" | custom-call | flops 77309411328 | bytes 50331648 | tf_op jit(solution)/shard_map/ffn/pallas_call | solution.py:121
  813.6 51.2 %combine.7 = f32[4096,2048]{1,0:T(8,128)} custom-call(s32[80]{0:T(128)} %get-tuple-element.53.wid, s32[80]{0:T(128)} %get-tuple-element.58.first, s32[80]{0:T(128)} %get-tuple-element.45.nval, s32[1]{0:T(128)} %bitcast.42.nblk, s32[16,4096]{1,0:T(8,128)} %get-tuple-element.27.pos_ref, f32[16,4096]{1,0:T(8,128)} %get-tuple-element.23.gate_ref, ...), custom_call_target="tpu_custom_call" | custom-call | flops 12884901888 | bytes 100663296 | tf_op jit(solution)/shard_map/combine/pallas_call | solution.py:182
  864.8 2.5 convert_element_type.57
  867.3 3.9 convert_element_type.58
  871.2 101.6 %reduce-scatter.9.cloned.1.call-done = f32[512,2048]{1,0:T(8,128)} async-done(((f32[4096,2048]{1,0:T(8,128)}), f32[512,2048]{1,0:T(8,128)}) %reduce-scatter.9.cloned.1.call-update) | async-done | bytes 4194320 | tf_op jit(solution)/shard_map/reduce_scatter | solution.py:286
  972.9 3.8 convert_element_type.59
  976.7 198.7 %reduce-scatter.11.cloned.1.call-done = f32[512,2048]{1,0:T(8,128)} async-done(((f32[4096,2048]{1,0:T(8,128)}), f32[512,2048]{1,0:T(8,128)}) %reduce-scatter.11.cloned.1.call-update) | async-done | bytes 4194320 | tf_op jit(solution)/shard_map/reduce_scatter | solution.py:286
  1175.4 2.5 convert_element_type.60
  1177.9 6.1 pad_maximum_fusion
  (104 shorter events, 17.1 us)
Async XLA Ops:
  6.5 95.9 %all-gather.7.cloned.1.call-start = ((), (), s32[]{:S(2)}) async-start(), calls=%async_computation.4 | async-start | bytes 18874368 | tf_op jit(solution)/shard_map/all_gather | solution.py:282
  12.5 2.2 copy-start
  12.5 14.4 %copy-start.5 = (s32[8]{0:T(128)S(1)}, s32[8]{0:T(128)}, u32[]{:S(2)}) copy-start(s32[8]{0:T(128)} %constant.122.clone) | copy-start | bytes 100
  12.5 281.0 %all-gather.9.cloned.1.call-start = ((), (), s32[]{:S(2)}) async-start(), calls=%async_computation.6 | async-start | bytes 18874368 | tf_op jit(solution)/shard_map/all_gather | solution.py:282
  12.6 25.4 %copy-start.1 = (bf16[2048,8]{0,1:T(8,128)(2,1)S(1)}, bf16[2048,8]{0,1:T(8,128)(2,1)}, u32[]{:S(2)}) copy-start(bf16[2048,8]{0,1:T(8,128)(2,1)} %param.9) | copy-start | bytes 98308
  13.3 471.1 %all-gather.11.cloned.1.call-start = ((), (), s32[]{:S(2)}) async-start(), calls=%async_computation.8 | async-start | bytes 18874368 | tf_op jit(solution)/shard_map/all_gather | solution.py:282
  14.0 661.3 %all-gather.13.cloned.1.call-start = ((), (), s32[]{:S(2)}) async-start(), calls=%async_computation.10 | async-start | bytes 18874368 | tf_op jit(solution)/shard_map/all_gather | solution.py:282
  14.6 850.2 %reduce-scatter.5.cloned.1.call-start = ((), (), s32[]{:S(2)}) async-start(), calls=%async_computation.5 | async-start | bytes 37748736 | tf_op jit(solution)/shard_map/reduce_scatter | solution.py:286
  292.1 0.7 copy-start.4
  292.1 575.2 %reduce-scatter.7.cloned.1.call-start = ((), (), s32[]{:S(2)}) async-start(), calls=%async_computation.7 | async-start | bytes 37748736 | tf_op jit(solution)/shard_map/reduce_scatter | solution.py:286
  483.0 0.7 copy-start.3
  483.0 489.9 %reduce-scatter.9.cloned.1.call-start = ((), (), s32[]{:S(2)}) async-start(), calls=%async_computation.9 | async-start | bytes 37748736 | tf_op jit(solution)/shard_map/reduce_scatter | solution.py:286
  673.9 0.7 copy-start.2
  673.9 501.5 %reduce-scatter.11.cloned.1.call-start = ((), (), s32[]{:S(2)}) async-start(), calls=%async_computation.11 | async-start | bytes 37748736 | tf_op jit(solution)/shard_map/reduce_scatter | solution.py:286
Sparse Core Ops, SparseCore 0:
  12.7 89.7 all-gather.6
  104.3 85.8 all-gather.8
  192.1 85.8 all-gather.10
  279.7 85.8 all-gather.12
  369.0 198.9 reduce-scatter.4
  571.4 198.9 reduce-scatter.6
  773.9 198.8 reduce-scatter.8
  976.4 198.9 reduce-scatter.10

commit v2 on v1

--- a/solution.py
+++ b/solution.py
@@ -8,23 +8,45 @@
 from jax.sharding import PartitionSpec as P
 
 CHUNKS = 4
+PIECES = {0: 1, 1: 1, 2: 2}
 GR = 16
 GB = 16
 BR = GR * GB
 WT = 512
 SP = 16
+SMEM = pl.BlockSpec(memory_space=pltpu.SMEM)
+HBM = pl.BlockSpec(memory_space=pltpu.HBM)
+VMEM_LIMIT = 56 * 2 ** 20
 
 
 def holder_list(p):
     return [0, (p // 2 + 1) % p, (p // 4 + 2) % p, (3 * p // 4 + 3) % p]
 
 
-def pack_kernel(wid, nblk, pos_ref, x_ref, o_ref, *, slots):
-    j = pl.program_id(0)
-
-    @pl.when(j < nblk[0])
-    def _():
-        pack_block(j, pos_ref, x_ref, o_ref, slots)
+def pack_kernel(wid, nblk, pos, xa, xb, o, *, slots, half, m, r):
+    d = xa.shape[1]
+
+    def body(pos_ref, xa_ref, xb_ref, o_ref):
+        j = pl.program_id(0)
+
+        @pl.when(wid[j] < half)
+        def _():
+            pack_block(j, pos_ref, xa_ref, o_ref, slots)
+
+        @pl.when(wid[j] >= half)
+        def _():
+            pack_block(j, pos_ref, xb_ref, o_ref, slots)
+
+    pltpu.emit_pipeline(
+        body,
+        grid=(nblk[0],),
+        in_specs=[
+            pl.BlockSpec((SP, WT), lambda j: (0, wid[j])),
+            pl.BlockSpec((WT, d), lambda j: (jnp.minimum(wid[j], half - 1) * m + r, 0)),
+            pl.BlockSpec((WT, d), lambda j: (jnp.maximum(wid[j] - half, 0) * m + r, 0)),
+        ],
+        out_specs=[pl.BlockSpec((GB, GR, d), lambda j: (j, 0, 0))],
+    )(pos, xa, xb, o)
 
 
 def pack_block(j, pos_ref, x_ref, o_ref, slots):
@@ -34,38 +56,43 @@
         oh = jnp.logical_or(oh, pos_ref[s:s + 1, :] == rows)
     oh = jnp.where(oh, 1.0, 0.0).astype(jnp.bfloat16)
     d = x_ref.shape[1]
-    step = 512
-    for n in range(0, d, step):
-        r = jnp.dot(oh, x_ref[:, n:n + step], preferred_element_type=jnp.float32)
-        o_ref[:, :, n:n + step] = r.astype(jnp.bfloat16).reshape(GB, GR, step)
-
-
-def pack(wid, nblk, pos, x, ng, slots):
-    d = x.shape[1]
+    step = 1024
+
+    @pl.loop(0, d // step)
+    def _(n):
+        col = pl.ds(pl.multiple_of(n * step, step), step)
+        r = jnp.dot(oh, x_ref[:, col], preferred_element_type=jnp.float32)
+        o_ref[:, :, col] = r.astype(jnp.bfloat16).reshape(GB, GR, step)
+
+
+def pack(wid, nblk, pos, xa, xb, ng, slots, m, r):
+    d = xa.shape[1]
+    half = xa.shape[0] // (m * WT)
     return pl.pallas_call(
-        functools.partial(pack_kernel, slots=slots),
-        grid_spec=pltpu.PrefetchScalarGridSpec(
-            num_scalar_prefetch=2,
-            grid=wid.shape,
-            in_specs=[
-                pl.BlockSpec((SP, WT), lambda j, wid, nb: (0, wid[j])),
-                pl.BlockSpec((WT, d), lambda j, wid, nb: (wid[j], 0)),
-            ],
-            out_specs=pl.BlockSpec((GB, GR, d), lambda j, wid, nb: (jnp.minimum(j, nb[0] - 1), 0, 0)),
-        ),
+        functools.partial(pack_kernel, slots=slots, half=half, m=m, r=r),
+        in_specs=[SMEM, SMEM, HBM, HBM, HBM],
+        out_specs=HBM,
         out_shape=jax.ShapeDtypeStruct((ng, GR, d), jnp.bfloat16),
         cost_estimate=pl.CostEstimate(flops=2 * 24 * BR * WT * d, bytes_accessed=24 * BR * d * 4, transcendentals=0),
         name="pack",
-    )(wid, nblk, pos, x)
+    )(wid, nblk, pos, xa, xb)
 
 
 def ffn_kernel(bexp, grp, nb, xs, w1, w3, w2, o, xbuf, obuf, abuf, isem, osem):
-    i = pl.program_id(0)
-    n = nb[0]
-
-    @pl.when(i < n)
-    def _():
-        ffn_block(i, n, grp, xs, w1, w3, w2, o, xbuf, obuf, abuf, isem, osem)
+    d, ff = w1.shape[1:]
+
+    def body(w1_ref, w3_ref, w2_ref):
+        ffn_block(pl.program_id(0), nb[0], grp, xs, w1_ref, w3_ref, w2_ref, o, xbuf, obuf, abuf, isem, osem)
+
+    pltpu.emit_pipeline(
+        body,
+        grid=(nb[0],),
+        in_specs=[
+            pl.BlockSpec((1, d, ff), lambda i: (bexp[i], 0, 0)),
+            pl.BlockSpec((1, d, ff), lambda i: (bexp[i], 0, 0)),
+            pl.BlockSpec((1, ff, d), lambda i: (bexp[i], 0, 0)),
+        ],
+    )(w1, w3, w2)
 
 
 def ffn_block(i, n, grp, xs, w1, w3, w2, o, xbuf, obuf, abuf, isem, osem):
@@ -120,41 +147,42 @@
     ff = w1.shape[2]
     return pl.pallas_call(
         ffn_kernel,
-        grid_spec=pltpu.PrefetchScalarGridSpec(
-            num_scalar_prefetch=3,
-            grid=bexp.shape,
-            in_specs=[
-                pl.BlockSpec(memory_space=pl.ANY),
-                pl.BlockSpec((1, d, ff), lambda i, be, gr, nb: (be[i], 0, 0)),
-                pl.BlockSpec((1, d, ff), lambda i, be, gr, nb: (be[i], 0, 0)),
-                pl.BlockSpec((1, ff, d), lambda i, be, gr, nb: (be[i], 0, 0)),
-            ],
-            out_specs=pl.BlockSpec(memory_space=pl.ANY),
-            scratch_shapes=[
-                pltpu.VMEM((2, GB, GR, d), jnp.bfloat16),
-                pltpu.VMEM((2, GB, GR, d), jnp.bfloat16),
-                pltpu.VMEM((BR, ff), jnp.bfloat16),
-                pltpu.SemaphoreType.DMA((2,)),
-                pltpu.SemaphoreType.DMA((2,)),
-            ],
-        ),
+        in_specs=[SMEM, SMEM, SMEM, HBM, HBM, HBM, HBM],
+        out_specs=HBM,
+        scratch_shapes=[
+            pltpu.VMEM((2, GB, GR, d), jnp.bfloat16),
+            pltpu.VMEM((2, GB, GR, d), jnp.bfloat16),
+            pltpu.VMEM((BR, ff), jnp.bfloat16),
+            pltpu.SemaphoreType.DMA((2,)),
+            pltpu.SemaphoreType.DMA((2,)),
+        ],
         out_shape=jax.ShapeDtypeStruct((ng, GR, d), jnp.bfloat16),
-        compiler_params=pltpu.CompilerParams(vmem_limit_bytes=56 * 2 ** 20),
+        compiler_params=pltpu.CompilerParams(vmem_limit_bytes=VMEM_LIMIT),
         cost_estimate=pl.CostEstimate(flops=6 * 24 * BR * d * ff, bytes_accessed=24 * BR * d * 4, transcendentals=0),
         name="ffn",
     )(bexp, grp, nb, xs, w1, w3, w2)
 
 
-def combine_kernel(wid, first, nval, nblk, pos_ref, gate_ref, o_ref, y_ref, *, slots):
-    j = pl.program_id(0)
-
-    @pl.when(j < nblk[0])
-    def _():
-        combine_block(j, first, nval, pos_ref, gate_ref, o_ref, y_ref, slots)
-
-
-def combine_block(j, first, nval, pos_ref, gate_ref, o_ref, y_ref, slots):
-    rows = lax.broadcasted_iota(jnp.int32, (BR, WT), 0) + j * BR
+def combine_kernel(wid, first, nval, nblk, off, pos, gate, o, y, *, slots, w0):
+    d = y.shape[1]
+
+    def body(pos_ref, gate_ref, o_ref, y_ref):
+        combine_block(pl.program_id(0), off, first, nval, pos_ref, gate_ref, o_ref, y_ref, slots)
+
+    pltpu.emit_pipeline(
+        body,
+        grid=(nblk[0],),
+        in_specs=[
+            pl.BlockSpec((SP, WT), lambda j: (0, w0 + wid[j])),
+            pl.BlockSpec((SP, WT), lambda j: (0, w0 + wid[j])),
+            pl.BlockSpec((GB, GR, d), lambda j: (off[0] + j, 0, 0)),
+        ],
+        out_specs=[pl.BlockSpec((WT, d), lambda j: (wid[j], 0))],
+    )(pos, gate, o, y)
+
+
+def combine_block(j, off, first, nval, pos_ref, gate_ref, o_ref, y_ref, slots):
+    rows = lax.broadcasted_iota(jnp.int32, (BR, WT), 0) + (off[0] + j) * BR
     gm = jnp.zeros((BR, WT), jnp.float32)
     for s in range(slots):
         gm = jnp.where(pos_ref[s:s + 1, :] == rows, gate_ref[s:s + 1, :], gm)
@@ -162,39 +190,27 @@
     d = y_ref.shape[1]
     step = 512
     live = lax.broadcasted_iota(jnp.int32, (BR, step), 0) < nval[j]
-    for c in range(0, d, step):
-        o = o_ref[:, :, c:c + step].reshape(BR, step)
+    keep = first[j] == 0
+
+    @pl.loop(0, d // step)
+    def _(n):
+        col = pl.ds(pl.multiple_of(n * step, step), step)
+        o = o_ref[:, :, col].reshape(BR, step)
         o = jnp.where(live, o, jnp.zeros((), jnp.bfloat16))
         r = lax.dot_general(gm, o, (((0,), (0,)), ((), ())), preferred_element_type=jnp.float32)
-
-        @pl.when(first[j] == 1)
-        def _():
-            y_ref[:, c:c + step] = r
-
-        @pl.when(first[j] == 0)
-        def _():
-            y_ref[:, c:c + step] += r
-
-
-def combine(wid, first, nval, nblk, pos, gate, o, slots):
+        y_ref[:, col] = r + jnp.where(keep, y_ref[:, col], 0.0)
+
+
+def combine(wid, first, nval, nblk, off, pos, gate, o, slots, w0, t):
     d = o.shape[2]
-    t = pos.shape[1]
     return pl.pallas_call(
-        functools.partial(combine_kernel, slots=slots),
-        grid_spec=pltpu.PrefetchScalarGridSpec(
-            num_scalar_prefetch=4,
-            grid=wid.shape,
-            in_specs=[
-                pl.BlockSpec((SP, WT), lambda j, wid, f, v, nb: (0, wid[j])),
-                pl.BlockSpec((SP, WT), lambda j, wid, f, v, nb: (0, wid[j])),
-                pl.BlockSpec((GB, GR, d), lambda j, wid, f, v, nb: (jnp.minimum(j, nb[0] - 1), 0, 0)),
-            ],
-            out_specs=pl.BlockSpec((WT, d), lambda j, wid, f, v, nb: (wid[j], 0)),
-        ),
+        functools.partial(combine_kernel, slots=slots, w0=w0),
+        in_specs=[SMEM] * 5 + [HBM] * 3,
+        out_specs=HBM,
         out_shape=jax.ShapeDtypeStruct((t, d), jnp.float32),
         cost_estimate=pl.CostEstimate(flops=2 * 24 * BR * WT * d, bytes_accessed=24 * BR * d * 8, transcendentals=0),
         name="combine",
-    )(wid, first, nval, nblk, pos, gate, o)
+    )(wid, first, nval, nblk, off, pos, gate, o)
 
 
 def solution(mesh):
@@ -214,6 +230,9 @@
         nw = tch // WT
         me = lax.axis_index("ep")
         gme = jnp.array(table, jnp.int32)[me]
+        core = me % 2
+        teams = [[2 * i + c for i in range(p // 2)] for c in range(2)]
+        swap = [(i, i ^ 1) for i in range(p)]
 
         rmax = p * min(td * k // p, tc * k) + -(-tch // nh)
         gmax = rmax // GR + nw * slots
@@ -224,7 +243,9 @@
 
         def chunked(v):
             a = lax.all_gather(v.T, "ep", axis=1, tiled=False)
-            return a.reshape(k, p, nc, tc).transpose(0, 2, 1, 3).reshape(k, nc * tch)
+            a = a.reshape(k, p // 2, 2, nc, tc).transpose(0, 3, 2, 1, 4)
+            a = jnp.where(core == 0, a, a[:, :, ::-1])
+            return a.reshape(k, nc * tch)
         rt = chunked(ridx)
         gt = chunked(gates).astype(jnp.float32)
         s_id = jnp.arange(slots, dtype=jnp.int32)
@@ -251,13 +272,24 @@
         pos = jnp.pad(pos, ((0, SP - slots), (0, 0), (0, 0)), constant_values=-1)
         gate = jnp.pad(gate.reshape(slots, nc, tch), ((0, SP - slots), (0, 0), (0, 0)))
 
-        jb = jnp.arange(wbmax, dtype=jnp.int32)
-        wid = jnp.minimum(jnp.sum((jb[None, :, None] >= b_end[:, None, :]).astype(jnp.int32), axis=2), nw - 1)
-        ohw = wid[:, :, None] == jnp.arange(nw)
-        jrel = jb[None, :] - jnp.sum(jnp.where(ohw, b_off[:, None, :], 0), axis=2)
-        nval = jnp.clip(jnp.sum(jnp.where(ohw, g_w[:, None, :], 0), axis=2) * GR - jrel * BR, 0, BR)
-        first = (jrel == 0).astype(jnp.int32)
+        def blocks(bend, gw, njb):
+            n = bend.shape[-1]
+            jb = jnp.arange(njb, dtype=jnp.int32)
+            boff = bend - jnp.maximum((gw + GB - 1) // GB, 1)
+            w = jnp.minimum(jnp.sum((jb[:, None] >= bend[..., None, :]).astype(jnp.int32), axis=-1), n - 1)
+            oh = w[..., None] == jnp.arange(n)
+            jrel = jb - jnp.sum(jnp.where(oh, boff[..., None, :], 0), axis=-1)
+            nval = jnp.clip(jnp.sum(jnp.where(oh, gw[..., None, :], 0), axis=-1) * GR - jrel * BR, 0, BR)
+            return w, (jrel == 0).astype(jnp.int32), nval
+        wid, _, _ = blocks(b_end, g_w, wbmax)
         nblk = b_end[:, -1:]
+        nwh = nw // 2
+        hbmax = (p // 2 * min(td * k // p, tc * k) + tch // 2 // nh) // GR + nwh * slots
+        hbmax = hbmax // GB + nwh
+        h_end = jnp.cumsum(nb_w.reshape(nc, 2, nwh), axis=2)
+        hwid, first, nval = blocks(h_end, g_w.reshape(nc, 2, nwh), hbmax)
+        hblk = h_end[:, :, -1:]
+        hoff = jnp.concatenate([jnp.zeros_like(hblk[:, :1]), hblk[:, :1]], axis=1)
 
         w_end = jnp.cumsum(n_g, axis=1)
         tg = w_end[:, -1, :]
@@ -279,11 +311,19 @@
 
         ys = []
         for c in range(nc):
-            xa = lax.all_gather(x[c * tc:(c + 1) * tc], "ep", axis=0, tiled=True)
-            xs = pack(wid[c], nblk[c], pos[:, c], xa, ng, slots)
+            if c in PIECES:
+                c0, m = c, PIECES[c]
+                xa = lax.all_gather(x[c0 * tc:(c0 + m) * tc], "ep", axis=0, tiled=True, axis_index_groups=teams)
+                xb = lax.ppermute(xa, "ep", swap)
+            xs = pack(wid[c], nblk[c], pos[:, c], xa, xb, ng, slots, m, c - c0)
             o = ffn(bexp[c], grp[c], nb[c], xs, w1, w3, w2)
-            yp = combine(wid[c], first[c], nval[c], nblk[c], pos[:, c], gate[:, c], o, slots)
-            ys.append(lax.psum_scatter(yp, "ep", scatter_dimension=0, tiled=True).astype(jnp.bfloat16))
+
+            def part(h):
+                return combine(hwid[c, h], first[c, h], nval[c, h], hblk[c, h], hoff[c, h], pos[:, c], gate[:, c], o, slots, h * nwh, tch // 2)
+            there = lax.ppermute(part(1), "ep", swap)
+            yp = part(0) + there
+            y = lax.psum_scatter(yp, "ep", scatter_dimension=0, tiled=True, axis_index_groups=teams)
+            ys.append(y.astype(jnp.bfloat16))
         return jnp.concatenate(ys, axis=0)
 
     spec_t = P(("dp", "ep"), None)

time: 1200 us -> 1200 us (level)
  waiting for transfers between devices: 345 us -> 205 us
  other arithmetic: 27.1 us -> 101 us
  Pallas kernels: 758 us -> 812 us
    reduce_scatter x4, waiting for transfers between devices: 300 us -> 152 us  [local(): lax.psum_scatter(yp, 'ep', scatter_dimension=0, tiled=True, axis_index_gr...]
    add x0 -> x4, other arithmetic: none -> 69.9 us  [local(): yp = part(0) + there]
    pallas_call x12 -> x16, Pallas kernels: 758 us -> 812 us  [the longest x4 423 us: ffn(): pl.pallas_call(ffn_kernel, in_specs=[SMEM, SMEM, SMEM, HBM, HBM, HBM, HBM...]
    all_gather x4 -> x3, waiting for transfers between devices: 42.9 us -> 48.4 us  [local(): lax.all_gather(x[c0 * tc:(c0 + m) * tc], 'ep', axis=0, tiled=True, axis_i...]
  transfers between devices with their start and end apart: 8 -> 14, of which waited for: 3 -> 3; matrix products, arithmetic and copies ran while one was open for 3% -> 10% of each run, Pallas kernels for 64% -> 68%
where the time goes in v2:
time: 1200 us; the launch traced here: 1190 us
  Pallas kernels  812 us (68%)
  waiting for transfers between devices  205 us (17%)
  other arithmetic  101 us (8%)
  local copies, waits for them, and re-layouts  28.7 us (2%)
  blocking collectives  24.4 us (2%)
  between operations  14.9 us (1%)
    pallas_call x4, Pallas kernels, ffn(): pl.pallas_call(ffn_kernel, in_specs=[SMEM, SMEM, SMEM, HBM, HBM, HBM, HBM...  423 us
    pallas_call x8, Pallas kernels, combine(): pl.pallas_call(functools.partial(combine_kernel, slots=slots, w0=w0), in_...  212 us
    pallas_call x4, Pallas kernels, pack(): pl.pallas_call(functools.partial(pack_kernel, slots=slots, half=half, m=m...  177 us
    reduce_scatter x4, waiting for transfers between devices, local(): lax.psum_scatter(yp, 'ep', scatter_dimension=0, tiled=True, axis_index_gr...  152 us
    add x4, other arithmetic, local(): yp = part(0) + there  69.9 us
    all_gather x3, waiting for transfers between devices, local(): lax.all_gather(x[c0 * tc:(c0 + m) * tc], 'ep', axis=0, tiled=True, axis_i...  48.4 us
    all_gather x2, blocking collectives, chunked(): a = lax.all_gather(v.T, 'ep', axis=1, tiled=False)  24.4 us
  transfers between devices with their start and end apart: 14, of which 3 were waited for; matrix products, arithmetic and copies ran while one was open for 10% of the time, Pallas kernels for 68%

profile of v2, /device:TPU:0, one launch (start us, length us, event | category | flops | bytes accessed | tf_op | source)
XLA Modules:
  0.0 1189.7 jit_solution(15573955417095185386)
XLA Ops:
  6.5 4.9 fusion.32
  12.3 4.8 slice.288
  17.2 13.7 %all-gather = s32[8,16384]{1,0:T(8,128)S(1)} all-gather(s32[8,2048]{1,0:T(8,128)S(1)} %bitcast.162), channel_id=2, replica_groups=mesh['dp'=2,'ep'=8] {'ep'}, dimensions={1}, use_global_device_ids=true | all-gather | bytes 589824 | tf_op jit(solution)/shard_map/all_gather | solution.py:245
  38.8 10.7 all-gather.1
  52.5 48.4 %all-gather.8.cloned.1.call-done.xa = bf16[2048,2048]{1,0:T(8,128)(2,1)} async-done(((bf16[512,2048]{1,0:T(8,128)(2,1)}), bf16[2048,2048]{1,0:T(8,128)(2,1)}) %all-gather.8.cloned.1.call-update) | async-done | bytes 8388624 | tf_op jit(solution)/shard_map/all_gather | solution.py:316
  118.3 44.3 %pack.5.xs = bf16[1312,16,2048]{2,1,0:T(8,128)(2,1)} custom-call(s32[80]{0:T(128)} %get-tuple-element.67.wid, s32[1]{0:T(128)} %bitcast.38.nblk, s32[16,4096]{1,0:T(8,128)} %get-tuple-element.21.pos, bf16[2048,2048]{1,0:T(8,128)(2,1)} %all-gather.8.cloned.1.call-done.xa, bf16[2048,2048]{1,0:T(8,128)(2,1)} %collective-permute-done.2.xb), custom_call_target="tpu_custom_call" | custom-call | flops 12884901888 | bytes 50331648 | tf_op jit(solution)/shard_map/pack/pallas_call | solution.py:71
  162.7 105.9 %ffn.5.o = bf16[1312,16,2048]{2,1,0:T(8,128)(2,1)} custom-call(s32[81]{0:T(128)} %get-tuple-element.75.bexp, s32[1296]{0:T(1024)} %squeeze.225.grp, s32[1]{0:T(128)} %bitcast.36.nb, bf16[1312,16,2048]{2,1,0:T(8,128)(2,1)} %pack.5.xs, bf16[9,2048,1024]{2,1,0:T(8,128)(2,1)} %w1.7, bf16[9,2048,1024]{2,1,0:T(8,128)(2,1)} %w3.7, bf16[9,1024,2048]{2,1,0:T(8,128)(2,1)} %w2.7), custom_call_target="tpu_custom_call" | custom-call | flops 77309411328 | bytes 50331648 | tf_op jit(solution)/shard_map/ffn/pallas_call | solution.py:148
  268.6 26.9 %combine.11 = f32[2048,2048]{1,0:T(8,128)} custom-call(s32[40]{0:T(128)} %get-tuple-element.57.wid, s32[40]{0:T(128)} %get-tuple-element.78.first, s32[40]{0:T(128)} %get-tuple-element.41.nval, s32[1]{0:T(128)} %bitcast.42.nblk, s32[1]{0:T(128)} %bitcast.32.nblk.off, s32[16,4096]{1,0:T(8,128)} %get-tuple-element.21.pos, f32[16,4096]{1,0:T(8,128)} %get-tuple-element.17.gate, ...), custom_call_target="tpu_custom_call" | custom-call | flops 12884901888 | bytes 100663296 | tf_op jit(solution)/shard_map/combine/pallas_call | solution.py:206
  297.9 26.0 %combine.10 = f32[2048,2048]{1,0:T(8,128)} custom-call(s32[40]{0:T(128)} %get-tuple-element.58.wid, s32[40]{0:T(128)} %get-tuple-element.77.first, s32[40]{0:T(128)} %get-tuple-element.42.nval, s32[1]{0:T(128)} %bitcast.32.nblk.off, s32[1]{0:T(128)} %constant.143.clone.1.off, s32[16,4096]{1,0:T(8,128)} %get-tuple-element.21.pos, ...), custom_call_target="tpu_custom_call" | custom-call | flops 12884901888 | bytes 100663296 | tf_op jit(solution)/shard_map/combine/pallas_call | solution.py:206
  323.9 17.5 %add.236 = f32[2048,2048]{1,0:T(8,128)} add(f32[2048,2048]{1,0:T(8,128)} %combine.10, f32[2048,2048]{1,0:T(8,128)} %collective-permute-done.3) | non-fusion elementwise | flops 4194304 | bytes 50331648 | tf_op jit(solution)/shard_map/add | solution.py:324
  342.8 44.3 %pack.4.xs = bf16[1312,16,2048]{2,1,0:T(8,128)(2,1)} custom-call(s32[80]{0:T(128)} %get-tuple-element.64.wid, s32[1]{0:T(128)} %bitcast.24.nblk, s32[16,4096]{1,0:T(8,128)} %get-tuple-element.20.pos, bf16[2048,2048]{1,0:T(8,128)(2,1)} %all-gather.6.cloned.1.call-done.xa, bf16[2048,2048]{1,0:T(8,128)(2,1)} %collective-permute-done.xb), custom_call_target="tpu_custom_call" | custom-call | flops 12884901888 | bytes 50331648 | tf_op jit(solution)/shard_map/pack/pallas_call | solution.py:71
  387.1 105.7 %ffn.4.o = bf16[1312,16,2048]{2,1,0:T(8,128)(2,1)} custom-call(s32[81]{0:T(128)} %get-tuple-element.72.bexp, s32[1296]{0:T(1024)} %squeeze.210.grp, s32[1]{0:T(128)} %bitcast.22.nb, bf16[1312,16,2048]{2,1,0:T(8,128)(2,1)} %pack.4.xs, bf16[9,2048,1024]{2,1,0:T(8,128)(2,1)} %w1.7, bf16[9,2048,1024]{2,1,0:T(8,128)(2,1)} %w3.7, bf16[9,1024,2048]{2,1,0:T(8,128)(2,1)} %w2.7), custom_call_target="tpu_custom_call" | custom-call | flops 77309411328 | bytes 50331648 | tf_op jit(solution)/shard_map/ffn/pallas_call | solution.py:148
  492.9 26.8 %combine.9 = f32[2048,2048]{1,0:T(8,128)} custom-call(s32[40]{0:T(128)} %get-tuple-element.52.wid, s32[40]{0:T(128)} %get-tuple-element.83.first, s32[40]{0:T(128)} %get-tuple-element.36.nval, s32[1]{0:T(128)} %bitcast.28.nblk, s32[1]{0:T(128)} %bitcast.10.nblk.off, s32[16,4096]{1,0:T(8,128)} %get-tuple-element.20.pos, f32[16,4096]{1,0:T(8,128)} %get-tuple-element.16.gate, ...), custom_call_target="tpu_custom_call" | custom-call | flops 12884901888 | bytes 100663296 | tf_op jit(solution)/shard_map/combine/pallas_call | solution.py:206
  520.2 26.0 %combine.8 = f32[2048,2048]{1,0:T(8,128)} custom-call(s32[40]{0:T(128)} %get-tuple-element.59.wid, s32[40]{0:T(128)} %get-tuple-element.76.first, s32[40]{0:T(128)} %get-tuple-element.43.nval, s32[1]{0:T(128)} %bitcast.10.nblk.off, s32[1]{0:T(128)} %constant.143.clone.1.off, s32[16,4096]{1,0:T(8,128)} %get-tuple-element.20.pos, ...), custom_call_target="tpu_custom_call" | custom-call | flops 12884901888 | bytes 100663296 | tf_op jit(solution)/shard_map/combine/pallas_call | solution.py:206
  546.2 17.5 %add.235 = f32[2048,2048]{1,0:T(8,128)} add(f32[2048,2048]{1,0:T(8,128)} %combine.8, f32[2048,2048]{1,0:T(8,128)} %collective-permute-done.1) | non-fusion elementwise | flops 4194304 | bytes 50331648 | tf_op jit(solution)/shard_map/add | solution.py:324
  565.1 3.7 collective-permute-done.4.xb
  568.8 44.4 %pack.7.xs = bf16[1312,16,2048]{2,1,0:T(8,128)(2,1)} custom-call(s32[80]{0:T(128)} %get-tuple-element.65.wid, s32[1]{0:T(128)} %bitcast.66.nblk, s32[16,4096]{1,0:T(8,128)} %get-tuple-element.23.pos, bf16[4096,2048]{1,0:T(8,128)(2,1)} %all-gather.10.cloned.1.call-done.xa, bf16[4096,2048]{1,0:T(8,128)(2,1)} %collective-permute-done.4.xb), custom_call_target="tpu_custom_call" | custom-call | flops 12884901888 | bytes 50331648 | tf_op jit(solution)/shard_map/pack/pallas_call | solution.py:71
  613.1 106.0 %ffn.7.o = bf16[1312,16,2048]{2,1,0:T(8,128)(2,1)} custom-call(s32[81]{0:T(128)} %get-tuple-element.73.bexp, s32[1296]{0:T(1024)} %squeeze.255.grp, s32[1]{0:T(128)} %bitcast.64.nb, bf16[1312,16,2048]{2,1,0:T(8,128)(2,1)} %pack.7.xs, bf16[9,2048,1024]{2,1,0:T(8,128)(2,1)} %w1.7, bf16[9,2048,1024]{2,1,0:T(8,128)(2,1)} %w3.7, bf16[9,1024,2048]{2,1,0:T(8,128)(2,1)} %w2.7), custom_call_target="tpu_custom_call" | custom-call | flops 77309411328 | bytes 50331648 | tf_op jit(solution)/shard_map/ffn/pallas_call | solution.py:148
  719.1 26.8 %combine.15 = f32[2048,2048]{1,0:T(8,128)} custom-call(s32[40]{0:T(128)} %get-tuple-element.53.wid, s32[40]{0:T(128)} %get-tuple-element.82.first, s32[40]{0:T(128)} %get-tuple-element.37.nval, s32[1]{0:T(128)} %bitcast.70.nblk, s32[1]{0:T(128)} %bitcast.60.nblk.off, s32[16,4096]{1,0:T(8,128)} %get-tuple-element.23.pos, f32[16,4096]{1,0:T(8,128)} %get-tuple-element.19.gate, ...), custom_call_target="tpu_custom_call" | custom-call | flops 12884901888 | bytes 100663296 | tf_op jit(solution)/shard_map/combine/pallas_call | solution.py:206
  745.9 26.1 %combine.14 = f32[2048,2048]{1,0:T(8,128)} custom-call(s32[40]{0:T(128)} %get-tuple-element.54.wid, s32[40]{0:T(128)} %get-tuple-element.81.first, s32[40]{0:T(128)} %get-tuple-element.38.nval, s32[1]{0:T(128)} %bitcast.60.nblk.off, s32[1]{0:T(128)} %constant.143.clone.1.off, s32[16,4096]{1,0:T(8,128)} %get-tuple-element.23.pos, ...), custom_call_target="tpu_custom_call" | custom-call | flops 12884901888 | bytes 100663296 | tf_op jit(solution)/shard_map/combine/pallas_call | solution.py:206
  772.0 17.5 %add.238 = f32[2048,2048]{1,0:T(8,128)} add(f32[2048,2048]{1,0:T(8,128)} %combine.14, f32[2048,2048]{1,0:T(8,128)} %collective-permute-done.6) | non-fusion elementwise | flops 4194304 | bytes 50331648 | tf_op jit(solution)/shard_map/add | solution.py:324
  791.0 44.3 %pack.6.xs = bf16[1312,16,2048]{2,1,0:T(8,128)(2,1)} custom-call(s32[80]{0:T(128)} %get-tuple-element.66.wid, s32[1]{0:T(128)} %bitcast.52.nblk, s32[16,4096]{1,0:T(8,128)} %get-tuple-element.22.pos, bf16[4096,2048]{1,0:T(8,128)(2,1)} %all-gather.10.cloned.1.call-done.xa, bf16[4096,2048]{1,0:T(8,128)(2,1)} %collective-permute-done.4.xb), custom_call_target="tpu_custom_call" | custom-call | flops 12884901888 | bytes 50331648 | tf_op jit(solution)/shard_map/pack/pallas_call | solution.py:71
  835.3 105.8 %ffn.6.o = bf16[1312,16,2048]{2,1,0:T(8,128)(2,1)} custom-call(s32[81]{0:T(128)} %get-tuple-element.74.bexp, s32[1296]{0:T(1024)} %squeeze.240.grp, s32[1]{0:T(128)} %bitcast.50.nb, bf16[1312,16,2048]{2,1,0:T(8,128)(2,1)} %pack.6.xs, bf16[9,2048,1024]{2,1,0:T(8,128)(2,1)} %w1.7, bf16[9,2048,1024]{2,1,0:T(8,128)(2,1)} %w3.7, bf16[9,1024,2048]{2,1,0:T(8,128)(2,1)} %w2.7), custom_call_target="tpu_custom_call" | custom-call | flops 77309411328 | bytes 50331648 | tf_op jit(solution)/shard_map/ffn/pallas_call | solution.py:148
  941.1 26.9 %combine.13 = f32[2048,2048]{1,0:T(8,128)} custom-call(s32[40]{0:T(128)} %get-tuple-element.55.wid, s32[40]{0:T(128)} %get-tuple-element.80.first, s32[40]{0:T(128)} %get-tuple-element.39.nval, s32[1]{0:T(128)} %bitcast.56.nblk, s32[1]{0:T(128)} %bitcast.46.nblk.off, s32[16,4096]{1,0:T(8,128)} %get-tuple-element.22.pos, f32[16,4096]{1,0:T(8,128)} %get-tuple-element.18.gate, ...), custom_call_target="tpu_custom_call" | custom-call | flops 12884901888 | bytes 100663296 | tf_op jit(solution)/shard_map/combine/pallas_call | solution.py:206
  968.0 26.1 %combine.12 = f32[2048,2048]{1,0:T(8,128)} custom-call(s32[40]{0:T(128)} %get-tuple-element.56.wid, s32[40]{0:T(128)} %get-tuple-element.79.first, s32[40]{0:T(128)} %get-tuple-element.40.nval, s32[1]{0:T(128)} %bitcast.46.nblk.off, s32[1]{0:T(128)} %constant.143.clone.1.off, s32[16,4096]{1,0:T(8,128)} %get-tuple-element.22.pos, ...), custom_call_target="tpu_custom_call" | custom-call | flops 12884901888 | bytes 100663296 | tf_op jit(solution)/shard_map/combine/pallas_call | solution.py:206
  994.1 17.5 %add.237 = f32[2048,2048]{1,0:T(8,128)} add(f32[2048,2048]{1,0:T(8,128)} %combine.12, f32[2048,2048]{1,0:T(8,128)} %collective-permute-done.5) | non-fusion elementwise | flops 4194304 | bytes 50331648 | tf_op jit(solution)/shard_map/add | solution.py:324
  1011.6 2.5 convert_element_type.54
  1014.1 3.9 convert_element_type.53
  1018.0 3.8 convert_element_type.56
  1021.8 152.2 %reduce-scatter.9.cloned.1.call-done = f32[512,2048]{1,0:T(8,128)} async-done(((f32[2048,2048]{1,0:T(8,128)}), f32[512,2048]{1,0:T(8,128)}) %reduce-scatter.9.cloned.1.call-update) | async-done | bytes 4194320 | tf_op jit(solution)/shard_map/reduce_scatter | solution.py:325
  1174.0 2.5 convert_element_type.55
  1176.5 6.1 pad_maximum_fusion
  (134 shorter events, 35.6 us)
Async XLA Ops:
  6.5 94.3 %all-gather.8.cloned.1.call-start = ((), (), s32[]{:S(2)}) async-start(), calls=%async_computation.6 | async-start | bytes 10485760 | tf_op jit(solution)/shard_map/all_gather | solution.py:316
  11.4 5.7 copy-start
  11.5 286.4 %all-gather.6.cloned.1.call-start = ((), (), s32[]{:S(2)}) async-start(), calls=%async_computation.4 | async-start | bytes 10485760 | tf_op jit(solution)/shard_map/all_gather | solution.py:316
  12.2 19.5 %copy-start.5 = (s32[8]{0:T(128)S(1)}, s32[8]{0:T(128)}, u32[]{:S(2)}) copy-start(s32[8]{0:T(128)} %constant.147.clone) | copy-start | bytes 100
  12.2 26.5 %copy-start.1 = (bf16[2048,8]{0,1:T(8,128)(2,1)S(1)}, bf16[2048,8]{0,1:T(8,128)(2,1)}, u32[]{:S(2)}) copy-start(bf16[2048,8]{0,1:T(8,128)(2,1)} %param.9) | copy-start | bytes 98308
  12.2 507.4 %all-gather.10.cloned.1.call-start = ((), (), s32[]{:S(2)}) async-start(), calls=%async_computation.8 | async-start | bytes 20971520 | tf_op jit(solution)/shard_map/all_gather | solution.py:316
  17.1 994.5 %reduce-scatter.7.cloned.1.call-start = ((), (), s32[]{:S(2)}) async-start(), calls=%async_computation.7 | async-start | bytes 20971520 | tf_op jit(solution)/shard_map/reduce_scatter | solution.py:325
  100.9 17.5 %collective-permute-start.2 = (bf16[2048,2048]{1,0:T(8,128)(2,1)}, bf16[2048,2048]{1,0:T(8,128)(2,1)}, u32[]{:S(2)}, u32[]{:S(2)}) collective-permute-start(bf16[2048,2048]{1,0:T(8,128)(2,1)} %all-gather.8.cloned.1.call-done.xa), channel_id=1, source_target_pairs={{0,1},{1,0},{2,3},{3,2},{4,5},{5,4},{6,7},{7,6},{8,9},{9,8},{10,11... | collective-permute-start | bytes 25165832 | tf_op jit(solution)/shard_map/ppermute | solution.py:317
  295.5 28.4 %collective-permute-start.3 = (f32[2048,2048]{1,0:T(8,128)}, f32[2048,2048]{1,0:T(8,128)}, u32[]{:S(2)}, u32[]{:S(2)}) collective-permute-start(f32[2048,2048]{1,0:T(8,128)} %combine.11), channel_id=1, source_target_pairs={{0,1},{1,0},{2,3},{3,2},{4,5},{5,4},{6,7},{7,6},{8,9},{9,8},{10,11... | collective-permute-start | bytes 50331656 | tf_op jit(solution)/shard_map/ppermute | solution.py:323
  297.9 45.0 %collective-permute-start = (bf16[2048,2048]{1,0:T(8,128)(2,1)}, bf16[2048,2048]{1,0:T(8,128)(2,1)}, u32[]{:S(2)}, u32[]{:S(2)}) collective-permute-start(bf16[2048,2048]{1,0:T(8,128)(2,1)} %all-gather.6.cloned.1.call-done.xa), channel_id=1, source_target_pairs={{0,1},{1,0},{2,3},{3,2},{4,5},{5,4},{6,7},{7,6},{8,9},{9,8},{10,11... | collective-permute-start | bytes 25165832 | tf_op jit(solution)/shard_map/ppermute | solution.py:317
  341.3 0.7 copy-start.4
  341.4 672.8 %reduce-scatter.5.cloned.1.call-start = ((), (), s32[]{:S(2)}) async-start(), calls=%async_computation.5 | async-start | bytes 20971520 | tf_op jit(solution)/shard_map/reduce_scatter | solution.py:325
  519.7 26.5 %collective-permute-start.1 = (f32[2048,2048]{1,0:T(8,128)}, f32[2048,2048]{1,0:T(8,128)}, u32[]{:S(2)}, u32[]{:S(2)}) collective-permute-start(f32[2048,2048]{1,0:T(8,128)} %combine.9), channel_id=1, source_target_pairs={{0,1},{1,0},{2,3},{3,2},{4,5},{5,4},{6,7},{7,6},{8,9},{9,8},{10,11... | collective-permute-start | bytes 50331656 | tf_op jit(solution)/shard_map/ppermute | solution.py:323
  519.7 49.1 %collective-permute-start.4 = (bf16[4096,2048]{1,0:T(8,128)(2,1)}, bf16[4096,2048]{1,0:T(8,128)(2,1)}, u32[]{:S(2)}, u32[]{:S(2)}) collective-permute-start(bf16[4096,2048]{1,0:T(8,128)(2,1)} %all-gather.10.cloned.1.call-done.xa), channel_id=1, source_target_pairs={{0,1},{1,0},{2,3},{3,2},{4,5},{5,4},{6,7},{7,6},{8,9},{9,8},{10,11... | collective-permute-start | bytes 50331656 | tf_op jit(solution)/shard_map/ppermute | solution.py:317
  563.6 0.7 copy-start.3
  563.7 454.3 %reduce-scatter.11.cloned.1.call-start = ((), (), s32[]{:S(2)}) async-start(), calls=%async_computation.10 | async-start | bytes 20971520 | tf_op jit(solution)/shard_map/reduce_scatter | solution.py:325
  745.9 26.1 %collective-permute-start.6 = (f32[2048,2048]{1,0:T(8,128)}, f32[2048,2048]{1,0:T(8,128)}, u32[]{:S(2)}, u32[]{:S(2)}) collective-permute-start(f32[2048,2048]{1,0:T(8,128)} %combine.15), channel_id=1, source_target_pairs={{0,1},{1,0},{2,3},{3,2},{4,5},{5,4},{6,7},{7,6},{8,9},{9,8},{10,11... | collective-permute-start | bytes 50331656 | tf_op jit(solution)/shard_map/ppermute | solution.py:323
  789.5 0.7 copy-start.2
  789.5 384.5 %reduce-scatter.9.cloned.1.call-start = ((), (), s32[]{:S(2)}) async-start(), calls=%async_computation.9 | async-start | bytes 20971520 | tf_op jit(solution)/shard_map/reduce_scatter | solution.py:325
  968.0 26.1 %collective-permute-start.5 = (f32[2048,2048]{1,0:T(8,128)}, f32[2048,2048]{1,0:T(8,128)}, u32[]{:S(2)}, u32[]{:S(2)}) collective-permute-start(f32[2048,2048]{1,0:T(8,128)} %combine.13), channel_id=1, source_target_pairs={{0,1},{1,0},{2,3},{3,2},{4,5},{5,4},{6,7},{7,6},{8,9},{9,8},{10,11... | collective-permute-start | bytes 50331656 | tf_op jit(solution)/shard_map/ppermute | solution.py:323
Sparse Core Ops, SparseCore 0:
  11.6 89.2 all-gather.7
  102.7 83.6 all-gather.5
  188.1 153.6 all-gather.9
  344.7 149.7 reduce-scatter.6
  563.8 154.9 reduce-scatter.4
  789.6 158.8 reduce-scatter.10
  1011.7 162.2 reduce-scatter.8
